TPU v7x, 32 devices: a whole 2x2x4 slice. The times are simulated.
32 devices in a mesh: dp: 8 (over z, x), cand: 4 (over y, core).
Axes of the slice: x: 2, y: 2, z: 4, core: 2. Of those that a mesh axis runs over, the one named last changes fastest.
Arguments:
- hidden: bfloat16 [16, 32, 128, 768], P('dp', 'cand'), may hold values from -24 to 24
- attn_weight: bfloat16 [768, 3072], P('dp'), may hold values from -1 to 1
- norm_gain: float32 [768], replicated, may hold values from 0.2 to 4
- pos_bias: float32 [12, 128, 128], replicated, may hold values from -5 to 5
- score_weight: float32 [768], replicated, may hold values from -4 to 4
- pair_lengths: int32 [16, 32], P('dp', 'cand'), may hold values from 32 to 128
- labels: int32 [16, 32], P('dp', 'cand'), may hold values from 0 to 3
Outputs:
- update: float32 [768, 3072], P('dp')
- loss: float32 [16], P('dp')
All inputs are finite; a program needn't handle non-finite values.
Results may differ from a plain program's by a relative error of at most 0.017.
Values may be sent and summed in bfloat16 or wider, within the bound.
A program may use at most 128 MiB of HBM per device.

v0:
```python
import jax
import jax.numpy as jnp
from jax import lax
from jax.sharding import PartitionSpec as P

EPS = 1e-06


def rms_rows(values, gain):
    factor = lax.rsqrt(jnp.mean(values * values, axis=-1, keepdims=True) + EPS)
    return values * factor * gain


def attend(qkv, pos_bias, pair_len):
    batch, seq, triple = qkv.shape
    width = triple // 3
    heads = pos_bias.shape[0]
    head_size = width // heads
    parts = qkv.reshape(batch, seq, 3, heads, head_size)
    logits = jnp.einsum(
        "bqhd,bkhd->bhqk", parts[:, :, 0], parts[:, :, 1], preferred_element_type=jnp.float32
    )
    logits = logits + pos_bias[None]
    valid = jnp.arange(seq, dtype=jnp.int32)[None, :] < pair_len[:, None]
    logits = jnp.where(valid[:, None, None, :], logits, -1e30)
    highest = jnp.max(logits, axis=-1, keepdims=True)
    expo = jnp.exp(logits - highest)
    probs = (expo / jnp.sum(expo, axis=-1, keepdims=True)).astype(jnp.bfloat16)
    context = jnp.einsum(
        "bhqk,bkhd->bqhd", probs, parts[:, :, 2], preferred_element_type=jnp.float32
    )
    return context.astype(jnp.bfloat16).reshape(batch, seq, width)


def score_head(pooled, score_weight):
    return jnp.sum(rms_rows(pooled, 1.0) * score_weight, axis=-1)


def shards(hidden, attn_weight, norm_gain, pos_bias, score_weight, pair_lengths, labels):
    q_local, c_local, seq, width = hidden.shape
    weights = lax.all_gather(attn_weight, "dp", axis=0, tiled=True)
    tokens = hidden.reshape(q_local * c_local, seq, width)
    pair_len = pair_lengths.reshape(-1)
    values = tokens.astype(jnp.float32)
    normed = rms_rows(values, norm_gain).astype(jnp.bfloat16)
    flat_norm = normed.reshape(-1, width)
    qkv = jnp.dot(flat_norm, weights[:, : 3 * width], preferred_element_type=jnp.float32)
    qkv = qkv.astype(jnp.bfloat16).reshape(q_local * c_local, seq, 3 * width)
    context, attend_back = jax.vjp(lambda block: attend(block, pos_bias, pair_len), qkv)
    flat_ctx = context.reshape(-1, width)
    out_rows = values + jnp.dot(
        flat_ctx, weights[:, 3 * width :], preferred_element_type=jnp.float32
    ).reshape(values.shape)
    live = (jnp.arange(seq, dtype=jnp.int32)[None, :] < pair_len[:, None]).astype(jnp.float32)
    share = live / pair_len.astype(jnp.float32)[:, None]
    pooled = jnp.sum(out_rows * share[:, :, None], axis=1)
    flat_scores, head_back = jax.vjp(lambda vector: score_head(vector, score_weight), pooled)
    scores = flat_scores.reshape(q_local, c_local)
    target = jnp.exp(labels.astype(jnp.float32))
    highest = lax.pmax(jnp.max(scores, axis=1), "cand")
    expsum, target_sum, target_dot = lax.psum(
        (
            jnp.sum(jnp.exp(scores - highest[:, None]), axis=1),
            jnp.sum(target, axis=1),
            jnp.sum(target * scores, axis=1),
        ),
        "cand",
    )
    loss = highest + jnp.log(expsum) - target_dot / target_sum
    score_grad = jnp.exp(scores - highest[:, None]) / expsum[:, None] - target / target_sum[:, None]
    pooled_grad = head_back(score_grad.reshape(-1))[0]
    out_grad = (pooled_grad[:, None, :] * share[:, :, None]).astype(jnp.bfloat16)
    flat_out = out_grad.reshape(-1, width)
    context_grad = jnp.dot(flat_out, weights[:, 3 * width :].T, preferred_element_type=jnp.float32)
    context_grad = context_grad.astype(jnp.bfloat16).reshape(context.shape)
    qkv_grad = attend_back(context_grad)[0].reshape(-1, 3 * width)
    dims = (((0,), (0,)), ((), ()))
    first = lax.dot_general(flat_norm, qkv_grad, dims, preferred_element_type=jnp.float32)
    second = lax.dot_general(flat_ctx, flat_out, dims, preferred_element_type=jnp.float32)
    shard = lax.psum_scatter(
        jnp.concatenate([first, second], axis=1).astype(jnp.bfloat16),
        "dp",
        scatter_dimension=0,
        tiled=True,
    ).astype(jnp.float32)
    shard = lax.psum(shard.astype(jnp.bfloat16), "cand").astype(jnp.float32)
    squares = lax.psum(jnp.sum(shard * shard), "dp")
    rms_value = jnp.sqrt(squares / (4.0 * width * width))
    update = shard / (rms_value + EPS)
    return (update, loss)


def solution(mesh):
    in_specs = (
        P("dp", "cand", None, None),
        P("dp", None),
        P(),
        P(),
        P(),
        P("dp", "cand"),
        P("dp", "cand"),
    )
    out_specs = (P("dp", None), P("dp"))
    return jax.shard_map(shards, mesh=mesh, in_specs=in_specs, out_specs=out_specs, check_vma=False)
```

profile of v0, /device:TPU:0, one launch (start us, length us, event | category | flops | bytes accessed | tf_op | source)
XLA Modules:
  0.0 460.7 jit_solution(10536083495842605806)
XLA Ops:
  7.2 0.7 all-gather.2.cloned.1.call-update
  8.0 0.9 lt.33
  8.9 2.3 copy.24
  11.3 2.6 multiply_reduce_fusion
  13.9 2.5 multiply_convert_fusion.1
  16.4 2.4 fusion.13
  18.8 73.4 %all-gather.2.cloned.1.call-done = bf16[768,3072]{1,0:T(8,128)(2,1)} async-done(((bf16[96,3072]{1,0:T(8,128)(2,1)}), bf16[768,3072]{1,0:T(8,128)(2,1)}) %all-gather.2.cloned.1.call-update) | async-done | bytes 4718608 | tf_op jit(solution)/shard_map/all_gather | solution.py:41
  92.3 12.5 %convolution_convert_fusion = bf16[2048,2304]{1,0:T(8,128)(2,1)} fusion(bf16[2048,768]{1,0:T(8,128)(2,1)} %fusion.13, bf16[768,3072]{1,0:T(8,128)(2,1)} %all-gather.2.cloned.1.call-done), kind=kOutput, calls=%fused_computation.11 | convolution fusion | flops 7252475904 | bytes 16121856 | tf_op jit(solution)/shard_map/dot_general | solution.py:47
  104.8 12.7 %copy.20 = bf16[2048,2304]{0,1:T(8,128)(2,1)} copy(bf16[2048,2304]{1,0:T(8,128)(2,1)} %convolution_convert_fusion) | data formatting | bytes 18874368 | tf_op jit(solution)/shard_map/convert_element_type | solution.py:48
  117.5 10.9 %copy.45 = bf16[288,8,16,128]{3,2,1,0:T(8,128)(2,1)} copy(bf16[288,8,16,128]{3,1,2,0:T(8,128)(2,1)} %bitcast.104) | data formatting | bytes 18874368
  128.4 6.4 %fusion.56 = (bf16[16,128,1,12,64]{1,0,4,3,2:T(8,128)(2,1)}, bf16[16,128,1,12,64]{1,0,4,3,2:T(8,128)(2,1)}, bf16[16,128,1,12,64]{1,0,4,3,2:T(8,128)(2,1)S(1)}) fusion(bf16[16,128,3,12,64]{1,0,4,3,2:T(8,128)(2,1)} %bitcast.103), kind=kLoop, calls=%fused_computation.91 | loop fusion | bytes 18874368 | tf_op jit(solution)/shard_map/jvp()/slice | solution.py:30
  134.8 7.5 %fusion.5 = (f32[16,12,128]{2,1,0:T(8,128)S(1)}, f32[16,12,128,128]{2,3,1,0:T(8,128)S(1)}) fusion(f32[12,128,128]{1,2,0:T(8,128)S(1)} %copy-done.11, pred[16,128]{1,0:T(8,128)(4,1)S(1)} %iota_compare_fusion, bf16[16,128,1,12,64]{1,0,4,3,2:T(8,128)(2,1)S(1)} %get-tuple-element.15, bf16[16,128,1,12,64]{1,0,4,3,2:T(8,128)(2,1)} %get-tuple-element.14), kind=kOutput, calls=%fused_computation.13 | convolution fusion | flops 412065792 | bytes 19761152 | tf_op jit(solution)/shard_map/jvp(bqhd,bkhd->bhqk)/dot_general | solution.py:20
  142.3 3.4 fusion.37
  145.7 1.2 copy-done
  146.9 8.1 %convert_reduce_fusion = (f32[16,12,128]{2,1,0:T(8,128)S(1)}, pred[16,12,128,128]{2,3,1,0:T(32,128)(4,1)}, bf16[16,12,128,128]{2,3,1,0:T(8,128)(2,1)S(1)}) fusion(f32[16,12,128]{2,1,0:T(8,128)S(1)} %get-tuple-element.20, f32[16,12,128,128]{2,3,1,0:T(8,128)S(1)} %get-tuple-element.21, f32[12,128,128]{1,2,0:T(8,128)S(1)} %copy-done.11, ...), kind=kLoop, calls=%fused_computation.7 | loop fusion | flops 25141248 | bytes 23103488 | tf_op jit(solution)/shard_map/jvp()/reduce_sum | solution.py:26
  155.0 2.7 fusion.36
  157.7 0.4 copy-done.2
  158.2 1.0 copy-done.6
  159.2 4.6 fusion.15
  164.3 5.7 %pmax.7 = f32[2]{0:T(128)S(1)} all-reduce(f32[2]{0:T(128)S(1)} %reduce_max.19), channel_id=1, replica_groups=mesh['dp'=8,'cand'=4] {'cand'}, use_global_device_ids=true, to_apply=%region_7.8 | all-reduce | flops 2 | bytes 16 | tf_op jit(solution)/shard_map/pmax | solution.py:60
  170.2 6.6 %all-reduce.3 = (f32[2]{0:T(128)S(1)}, f32[2]{0:T(128)S(1)}, f32[2]{0:T(128)S(1)}) all-reduce(f32[2]{0:T(128)S(1)} %get-tuple-element.3, f32[2]{0:T(128)S(1)} %get-tuple-element.4, f32[2]{0:T(128)S(1)} %get-tuple-element.2), channel_id=1, replica_groups=mesh['dp'=8,'cand'=4] {'cand'}, use_global_device_ids=true, to_apply=%region_11.12 | all-reduce | flops 6 | bytes 48 | tf_op jit(solution)/shard_map/psum | solution.py:61
  177.0 0.2 fusion.45
  177.3 0.4 fusion.11
  177.7 5.3 %convolution_convert_fusion.2 = bf16[2048,768]{1,0:T(8,128)(2,1)} fusion(bf16[2048,768]{1,0:T(8,128)(2,1)S(1)} %fusion.11, bf16[768,3072]{1,0:T(8,128)(2,1)} %all-gather.2.cloned.1.call-done), kind=kOutput, calls=%fused_computation.41 | convolution fusion | flops 2417491968 | bytes 7471104 | tf_op jit(solution)/shard_map/dot_general | solution.py:74
  182.9 4.7 %copy.27 = bf16[2048,768]{0,1:T(8,128)(2,1)} copy(bf16[2048,768]{1,0:T(8,128)(2,1)} %convolution_convert_fusion.2) | data formatting | bytes 6291456 | tf_op jit(solution)/shard_map/convert_element_type | solution.py:75
  187.7 2.9 copy.46
  190.6 1.6 copy-done.13
  192.2 9.0 %convert_bitcast_fusion.2 = bf16[16,128,1,12,64]{1,4,3,0,2:T(8,128)(2,1)} fusion(bf16[16,12,128,128]{2,3,1,0:T(8,128)(2,1)} %copy-done.2, bf16[16,12,64,128]{3,0,2,1:T(8,128)(2,1)S(1)} %bitcast.108), kind=kOutput, calls=%fused_computation.50 | convolution fusion | flops 404226048 | bytes 12582912 | tf_op jit(solution)/shard_map/transpose(jvp(bhqk,bkhd->bqhd))/dot_general | solution.py:29
  201.2 12.6 %fusion.3 = (f32[16,12,128]{2,1,0:T(8,128)S(1)}, bf16[16,12,128,128]{2,3,1,0:T(8,128)(2,1)}) fusion(f32[16,12,128]{2,1,0:T(8,128)S(1)} %multiply_divide_fusion, f32[16,12,128]{2,1,0:T(8,128)S(1)} %get-tuple-element.20, f32[16,12,128,128]{2,3,1,0:T(8,128)} %copy-done, f32[12,128,128]{1,2,0:T(8,128)S(1)} %copy-done.11, ...), kind=kOutput, calls=%fused_computation.5 | convolution fusion | flops 427794432 | bytes 26249216 | tf_op jit(solution)/shard_map/transpose(jvp(bhqk,bkhd->bqhd))/dot_general | solution.py:29
  213.9 10.1 %fusion.53 = (f32[16,12,128]{2,1,0:T(8,128)S(1)}, f32[16,12,128,128]{2,3,1,0:T(8,128)}) fusion(f32[16,12,128]{2,1,0:T(8,128)S(1)} %get-tuple-element.20, f32[16,12,128,128]{2,3,1,0:T(8,128)S(1)} %bitcast.102, f32[12,128,128]{1,2,0:T(8,128)S(1)} %copy-done.11, pred[16,128]{1,0:T(8,128)(4,1)S(1)} %iota_compare_fusion, f32[16,12,128]{2,1,0:T(8,128)S(1)} %neg.9, ...), kind=kLoop, calls=%fused_computation.90 | loop fusion | flops 25141248 | bytes 32638976 | tf_op jit(solution)/shard_map/transpose(jvp())/reduce_sum | solution.py:27
  224.1 11.4 %convert_bitcast_fusion.1 = bf16[16,128,1,12,64]{1,4,3,0,2:T(8,128)(2,1)} fusion(bf16[16,128,1,12,64]{1,0,4,3,2:T(8,128)(2,1)} %get-tuple-element.14, f32[16,12,128,128]{2,3,1,0:T(8,128)} %get-tuple-element.9, pred[16,12,128,128]{2,3,1,0:T(32,128)(4,1)} %get-tuple-element.11, f32[16,12,128]{2,1,0:T(8,128)S(1)} %negate_divide_fusion, ...), kind=kOutput, calls=%fused_computation.49 | convolution fusion | flops 413663232 | bytes 22120448 | tf_op jit(solution)/shard_map/transpose(jvp(bqhd,bkhd->bhqk))/dot_general | solution.py:20
  235.5 0.5 copy-done.4
  235.9 1.0 copy-done.7
  237.0 4.2 convert_bitcast_fusion
  241.2 2.1 multiply_convert_fusion
  243.3 0.9 copy-done.12
  244.2 6.8 %pad_add_fusion = bf16[16,128,3,12,64]{1,4,3,0,2:T(8,128)(2,1)} fusion(bf16[16,128,1,12,64]{1,4,3,0,2:T(8,128)(2,1)} %convert_bitcast_fusion, bf16[16,128,1,12,64]{1,4,3,0,2:T(8,128)(2,1)} %convert_bitcast_fusion.1, bf16[16,128,1,12,64]{1,4,3,0,2:T(8,128)(2,1)S(1)} %copy-done.12), kind=kLoop, calls=%fused_computation.17 | loop fusion | flops 9437184 | bytes 18874368 | tf_op jit(solution)/shard_map/transpose(jvp())/add_any | solution.py:21
  251.0 26.1 %copy.33 = bf16[16,128,3,12,64]{1,0,4,3,2:T(8,128)(2,1)} copy(bf16[16,128,3,12,64]{1,4,3,0,2:T(8,128)(2,1)} %pad_add_fusion) | data formatting | bytes 18874368 | tf_op jit(solution)/shard_map/transpose(jvp())/add_any | solution.py:21
  277.2 2.4 copy.34
  279.6 11.4 %fusion.22 = bf16[768,2304]{1,0:T(8,128)(2,1)S(1)} fusion(bf16[2048,768]{1,0:T(8,128)(2,1)S(1)} %bitcast.113, bf16[288,8,16,128]{3,2,1,0:T(8,128)(2,1)} %bitcast.110), kind=kOutput, calls=%fused_computation.37 | convolution fusion | flops 7249526784 | bytes 16121856 | tf_op jit(solution)/shard_map/dot_general | solution.py:78
  291.0 2.6 fusion.38
  293.7 2.8 pad_maximum_fusion
  296.5 94.1 %reduce-scatter.2.cloned.1.call-done = bf16[96,3072]{1,0:T(8,128)(2,1)} async-done(((bf16[768,3072]{1,0:T(8,128)(2,1)}), bf16[96,3072]{1,0:T(8,128)(2,1)}) %reduce-scatter.2.cloned.1.call-update) | async-done | bytes 589840 | tf_op jit(solution)/shard_map/reduce_scatter | solution.py:80
  390.6 35.8 %all-reduce.6.cloned.1.call-done = bf16[96,3072]{1,0:T(8,128)(2,1)} async-done(((bf16[96,3072]{1,0:T(8,128)(2,1)}), bf16[96,3072]{1,0:T(8,128)(2,1)}) %all-reduce.6.cloned.1.call-update) | async-done | bytes 589840 | tf_op jit(solution)/shard_map/psum | solution.py:86
  426.4 2.0 fusion.41
  428.4 0.5 divide_subtract_fusion.1
  428.9 22.0 %psum.38 = f32[]{:T(128)} all-reduce(f32[]{:T(128)} %fusion.41), channel_id=1, replica_groups=mesh['dp'=8,'cand'=4] {'dp'}, use_global_device_ids=true, to_apply=%region_19.20 | all-reduce | flops 1 | bytes 8 | tf_op jit(solution)/shard_map/psum | solution.py:87
  451.6 2.2 convert_divide_fusion.1
  (60 shorter events, 1.4 us)
Async XLA Ops:
  7.2 6.8 %copy-start.5 = (bf16[2,8,128,768]{3,2,1,0:T(8,128)(2,1)S(1)}, bf16[2,8,128,768]{3,2,1,0:T(8,128)(2,1)}, u32[]{:S(2)}) copy-start(bf16[2,8,128,768]{3,2,1,0:T(8,128)(2,1)} %param.7) | copy-start | bytes 9437188
  7.2 6.8 %copy-start.17 = (f32[768]{0:T(1024)S(1)}, f32[768]{0:T(1024)}, u32[]{:S(2)}) copy-start(f32[768]{0:T(1024)} %param.9) | copy-start | bytes 9220
  7.2 85.1 %all-gather.2.cloned.1.call-start = ((), (), s32[]{:S(2)}) async-start(), calls=%async_computation.1 | async-start | bytes 5308416 | tf_op jit(solution)/shard_map/all_gather | solution.py:41
  7.9 382.7 %reduce-scatter.2.cloned.1.call-start = ((), (), s32[]{:S(2)}) async-start(), calls=%async_computation.2 | async-start | bytes 5308416 | tf_op jit(solution)/shard_map/reduce_scatter | solution.py:80
  128.4 6.4 %copy-start.11 = (f32[12,128,128]{1,2,0:T(8,128)S(1)}, f32[12,128,128]{1,2,0:T(8,128)}, u32[]{:S(2)}) copy-start(f32[12,128,128]{1,2,0:T(8,128)} %copy.24) | copy-start | bytes 2359300
  134.8 7.6 %copy-start.3 = (bf16[16,128,1,12,64]{1,0,4,3,2:T(8,128)(2,1)}, bf16[16,128,1,12,64]{1,0,4,3,2:T(8,128)(2,1)S(1)}, u32[]{:S(2)}) copy-start(bf16[16,128,1,12,64]{1,0,4,3,2:T(8,128)(2,1)S(1)} %get-tuple-element.15) | copy-start | bytes 9437188
  142.3 4.6 copy-start
  146.9 8.1 %copy-start.8 = (bf16[16,128,1,12,64]{1,0,4,3,2:T(8,128)(2,1)S(1)}, bf16[16,128,1,12,64]{1,0,4,3,2:T(8,128)(2,1)}, u32[]{:S(2)}) copy-start(bf16[16,128,1,12,64]{1,0,4,3,2:T(8,128)(2,1)} %get-tuple-element.13) | copy-start | bytes 9437188
  155.0 3.2 copy-start.2
  155.0 4.2 copy-start.6
  158.2 5.6 %copy-start.9 = (bf16[16,12,64,128]{3,2,1,0:T(8,128)(2,1)}, bf16[16,12,64,128]{3,2,1,0:T(8,128)(2,1)S(1)}, u32[]{:S(2)}) copy-start(bf16[16,12,64,128]{3,2,1,0:T(8,128)(2,1)S(1)} %fusion.36) | copy-start | bytes 9437188
  159.2 4.7 %copy-start.16 = (f32[768]{0:T(1024)S(1)}, f32[768]{0:T(1024)}, u32[]{:S(2)}) copy-start(f32[768]{0:T(1024)} %param.11) | copy-start | bytes 9220
  159.2 10.8 %copy-start.18 = (s32[2,8]{1,0:T(2,128)S(1)}, s32[2,8]{1,0:T(2,128)}, u32[]{:S(2)}) copy-start(s32[2,8]{1,0:T(2,128)} %param.13) | copy-start | bytes 196
  190.5 1.6 copy-start.13
  192.2 21.7 %slice-start = ((s8[12582912]{0:T(1024)(128)(4,1)}), s8[4194304]{0:T(1024)(128)(4,1)S(1)}, s32[]{:S(2)}) async-start(s8[12582912]{0:T(1024)(128)(4,1)} %bitcast.101), calls=%async_computation.4 | async-start | bytes 8388608
  201.2 12.7 %slice-start.1 = ((s8[12582912]{0:T(1024)(128)(4,1)}), s8[4194304]{0:T(1024)(128)(4,1)S(1)}, s32[]{:S(2)}) async-start(s8[12582912]{0:T(1024)(128)(4,1)} %bitcast.101), calls=%async_computation.5 | async-start | bytes 8388608
  201.2 12.7 %slice-start.2 = ((s8[12582912]{0:T(1024)(128)(4,1)}), s8[4194304]{0:T(1024)(128)(4,1)S(1)}, s32[]{:S(2)}) async-start(s8[12582912]{0:T(1024)(128)(4,1)} %bitcast.101), calls=%async_computation.6 | async-start | bytes 8388608
  224.1 11.4 %copy-start.1 = (f32[16,12,128,128]{2,3,1,0:T(8,128)S(1)}, f32[16,12,128,128]{2,3,1,0:T(8,128)}, u32[]{:S(2)}) copy-start(f32[16,12,128,128]{2,3,1,0:T(8,128)} %get-tuple-element.9) | copy-start | bytes 37748740
  224.1 11.8 %copy-start.4 = (bf16[16,128,1,12,64]{1,0,4,3,2:T(8,128)(2,1)S(1)}, bf16[16,128,1,12,64]{1,0,4,3,2:T(8,128)(2,1)}, u32[]{:S(2)}) copy-start(bf16[16,128,1,12,64]{1,0,4,3,2:T(8,128)(2,1)} %copy-done.3) | copy-start | bytes 9437188
  224.1 12.9 %copy-start.7 = (pred[16,12,128,128]{2,3,1,0:T(32,128)(4,1)S(1)}, pred[16,12,128,128]{2,3,1,0:T(32,128)(4,1)}, u32[]{:S(2)}) copy-start(pred[16,12,128,128]{2,3,1,0:T(32,128)(4,1)} %get-tuple-element.11) | copy-start | bytes 9437188
  241.2 3.0 copy-start.12
  251.0 26.2 %copy-start.10 = (bf16[16,12,64,128]{3,2,1,0:T(8,128)(2,1)S(1)}, bf16[16,12,64,128]{3,2,1,0:T(8,128)(2,1)}, u32[]{:S(2)}) copy-start(bf16[16,12,64,128]{3,2,1,0:T(8,128)(2,1)} %copy-done.9) | copy-start | bytes 9437188
  277.2 2.5 copy-start.15
  279.6 11.4 %copy-start.14 = (bf16[16,128,768]{2,1,0:T(8,128)(2,1)S(1)}, bf16[16,128,768]{2,1,0:T(8,128)(2,1)}, u32[]{:S(2)}) copy-start(bf16[16,128,768]{2,1,0:T(8,128)(2,1)} %multiply_convert_fusion) | copy-start | bytes 9437188
  296.5 130.0 %all-reduce.6.cloned.1.call-start = ((), (), s32[]{:S(2)}) async-start(), calls=%async_computation.3 | async-start | bytes 1179648 | tf_op jit(solution)/shard_map/psum | solution.py:86
Sparse Core Ops, SparseCore 0:
  10.2 82.0 all-gather.1
  296.6 93.9 reduce-scatter.1
  393.0 33.3 all-reduce.5
where the time goes:
time: 464 us; the launch traced here: 461 us
  waiting for transfers between devices  204 us (44%)
  matrix products  83.9 us (18%)
  local copies, waits for them, and re-layouts  76.2 us (16%)
  other arithmetic  47.1 us (10%)
  blocking collectives  34.2 us (7%)
  between operations  15.2 us (3%)
    reduce_scatter x1, waiting for transfers between devices, shards(): lax.psum_scatter(jnp.concatenate([first, second], axis=1).astype(jnp.bflo...  94.1 us
    all_gather x1, waiting for transfers between devices, shards(): weights = lax.all_gather(attn_weight, 'dp', axis=0, tiled=True)  73.4 us
    psum x1, waiting for transfers between devices, shards(): shard = lax.psum(shard.astype(jnp.bfloat16), 'cand').astype(jnp.float32)  35.8 us
    add_any x1, local copies, waits for them, and re-layouts, attend(): parts[:, :, 0]  26.1 us
    dot_general x3, matrix products, attend(): jnp.einsum('bhqk,bkhd->bqhd', probs, parts[:, :, 2], preferred_element_ty...  24.4 us
    dot_general x3, matrix products, attend(): jnp.einsum('bqhd,bkhd->bhqk', parts[:, :, 0], parts[:, :, 1], preferred_e...  23.1 us
    unnamed x47, local copies, waits for them, and re-layouts  22.7 us
    psum x1, blocking collectives, shards(): squares = lax.psum(jnp.sum(shard * shard), 'dp')  22 us
  transfers between devices with their start and end apart: 3, of which 3 were waited for; matrix products, arithmetic and copies ran while one was open for 2% of the time, Pallas kernels for 0%

commit v1 on v0

v1 whole, which is shorter than its diff:
```python
import functools

import jax
import jax.numpy as jnp
from jax import lax
from jax.experimental import pallas as pl
from jax.experimental.pallas import tpu as pltpu
from jax.sharding import PartitionSpec as P

EPS = 1e-06
F32 = jnp.float32
BF16 = jnp.bfloat16
VMEM_LIMIT = 60 * 1024 * 1024
NT = (((1,), (1,)), ((), ()))
TN = (((0,), (0,)), ((), ()))


def half_masks(lanes):
    lane = lax.broadcasted_iota(jnp.int32, (1, lanes), 1)
    low = (lane < lanes // 2).astype(F32)
    return low.astype(BF16), (1.0 - low).astype(BF16)


def stack_halves(block, low, high):
    return jnp.concatenate([block * low, block * high], axis=0)


def forward_kernel(hpad, len_ref, h_ref, gain_ref, w_ref, bias_ref, nt_ref, qk_ref, p_ref, u_ref, hsum_ref, norm_scr):
    batch, seq, width = h_ref.shape
    heads = bias_ref.shape[0]
    duo = 2 * (width // heads)
    step = pl.program_id(0)
    values = h_ref[...].reshape(batch * seq, width).astype(F32)
    factor = lax.rsqrt(jnp.mean(values * values, axis=-1, keepdims=True) + EPS)
    normed = (values * factor * gain_ref[...]).astype(BF16)
    norm_scr[...] = normed.reshape(batch, seq, width)
    nt_ref[...] = normed.T
    qk = jnp.dot(normed, w_ref[...], preferred_element_type=F32)
    qk_ref[...] = qk.astype(BF16).reshape(batch, seq, 2 * width)
    low, high = half_masks(duo)
    col = lax.broadcasted_iota(jnp.int32, (1, seq), 1)
    row = lax.broadcasted_iota(jnp.int32, (seq, 1), 0)

    def pair(i, carry):
        length = len_ref[step * batch + i]
        penalty = jnp.where(col < length, 0.0, 1.0) > 0.5
        live = row < length
        live2 = jnp.concatenate([live.astype(F32)] * 2, axis=0)
        sums = []
        for hp in range(heads // 2):
            q2 = qk_ref[i, :, hp * duo : (hp + 1) * duo]
            k2 = qk_ref[i, :, width + hp * duo : width + (hp + 1) * duo]
            logits = lax.dot_general(stack_halves(q2, low, high), k2, NT, preferred_element_type=F32)
            logits = logits + bias_ref[2 * hp : 2 * hp + 2].reshape(2 * seq, seq)
            logits = jnp.where(penalty, -1e30, logits)
            expo = jnp.exp(logits - jnp.max(logits, axis=-1, keepdims=True))
            inv = live2 / jnp.sum(expo, axis=-1, keepdims=True)
            probs = (expo * inv).astype(BF16)
            p_ref[i, 2 * hp : 2 * hp + 2] = probs.reshape(2, seq, seq)
            sums.append(jnp.sum(probs.astype(F32).reshape(2, seq, seq), axis=1))
        if hpad > heads:
            sums.append(jnp.zeros((hpad - heads, seq), F32))
        weights = jnp.concatenate(sums, axis=0).astype(BF16)
        u_ref[i] = jnp.dot(weights, norm_scr[i], preferred_element_type=F32).astype(BF16)
        rows = h_ref[i].astype(F32) * live.astype(F32)
        hsum_ref[i] = jnp.sum(rows, axis=0, keepdims=True)
        return carry

    lax.fori_loop(0, batch, pair, 0)


def forward(tokens, pair_len, gain, wqk, pos_bias):
    pairs, seq, width = tokens.shape
    heads = pos_bias.shape[0]
    hpad = -(-heads // 16) * 16
    batch = 4 if pairs % 4 == 0 else 1
    full = lambda *shape: pl.BlockSpec(shape, lambda i: (0,) * len(shape))
    return pl.pallas_call(
        functools.partial(forward_kernel, hpad),
        grid=(pairs // batch,),
        in_specs=[
            pl.BlockSpec(memory_space=pltpu.SMEM),
            pl.BlockSpec((batch, seq, width), lambda i: (i, 0, 0)),
            full(1, width),
            full(width, 2 * width),
            full(heads, seq, seq),
        ],
        out_specs=[
            pl.BlockSpec((width, batch * seq), lambda i: (0, i)),
            pl.BlockSpec((batch, seq, 2 * width), lambda i: (i, 0, 0)),
            pl.BlockSpec((batch, heads, seq, seq), lambda i: (i, 0, 0, 0)),
            pl.BlockSpec((batch, hpad, width), lambda i: (i, 0, 0)),
            pl.BlockSpec((batch, 1, width), lambda i: (i, 0, 0)),
        ],
        out_shape=[
            jax.ShapeDtypeStruct((width, pairs * seq), BF16),
            jax.ShapeDtypeStruct((pairs, seq, 2 * width), BF16),
            jax.ShapeDtypeStruct((pairs, heads, seq, seq), BF16),
            jax.ShapeDtypeStruct((pairs, hpad, width), BF16),
            jax.ShapeDtypeStruct((pairs, 1, width), F32),
        ],
        scratch_shapes=[pltpu.VMEM((batch, seq, width), BF16)],
        compiler_params=pltpu.CompilerParams(vmem_limit_bytes=VMEM_LIMIT),
        cost_estimate=pl.CostEstimate(flops=30_000_000_000, bytes_accessed=24_000_000, transcendentals=0),
        name="attend_forward",
    )(pair_len, tokens, gain, wqk, pos_bias)


def head_mask(hpad, width, head_size):
    lane = lax.broadcasted_iota(jnp.int32, (hpad, width), 1)
    head = lax.broadcasted_iota(jnp.int32, (hpad, width), 0)
    start = head * head_size
    return ((lane >= start) & (lane < start + head_size)).astype(F32)


def score_kernel(head_size, u_ref, wv_ref, wo_ref, hsum_ref, len_ref, sw_ref, ctx_ref, pooled_ref, score_ref):
    pairs, hpad, width = u_ref.shape
    mixed = jnp.dot(u_ref[...].reshape(pairs * hpad, width), wv_ref[...], preferred_element_type=F32)
    mask = head_mask(hpad, width, head_size)
    ctx = jnp.sum(mixed.reshape(pairs, hpad, width) * mask[None], axis=1)
    ctx_ref[...] = ctx.astype(BF16)
    share = 1.0 / len_ref[...]
    mean = ctx * share
    high = mean.astype(BF16)
    low = (mean - high.astype(F32)).astype(BF16)
    both = jnp.dot(jnp.concatenate([high, low], axis=0), wo_ref[...], preferred_element_type=F32)
    pooled = hsum_ref[...] * share + both[:pairs] + both[pairs:]
    pooled_ref[...] = pooled
    factor = lax.rsqrt(jnp.mean(pooled * pooled, axis=-1, keepdims=True) + EPS)
    score_ref[...] = jnp.sum(pooled * factor * sw_ref[...], axis=-1, keepdims=True)


def middle_kernel(head_size, sg_ref, pooled_ref, len_ref, sw_ref, u_ref, ctx_ref, wv_ref, wo_ref, wc_ref, gvo_ref):
    pairs, hpad, width = u_ref.shape
    pooled = pooled_ref[...]
    sw = sw_ref[...]
    factor = lax.rsqrt(jnp.mean(pooled * pooled, axis=-1, keepdims=True) + EPS)
    dot = jnp.sum(pooled * sw, axis=-1, keepdims=True) * (1.0 / width)
    grad = sg_ref[...] * (factor * sw - pooled * (factor * factor * factor * dot))
    out_grad = (grad / len_ref[...]).astype(BF16)
    cg = lax.dot_general(out_grad, wo_ref[...], NT, preferred_element_type=F32).astype(BF16).astype(F32)
    mask = head_mask(hpad, width, head_size)
    spread = (cg[:, None, :] * mask[None]).astype(BF16).reshape(pairs * hpad, width)
    wc = lax.dot_general(spread, wv_ref[...], NT, preferred_element_type=F32)
    wc_ref[...] = wc.astype(BF16).reshape(pairs, hpad, width)
    u = u_ref[...].reshape(pairs * hpad, width)
    gvo_ref[:, :width] = lax.dot_general(u, spread, TN, preferred_element_type=F32).astype(BF16)
    gvo_ref[:, width:] = lax.dot_general(ctx_ref[...], out_grad, TN, preferred_element_type=F32).astype(BF16)


def backward_kernel(nt_ref, q_ref, k_ref, p_ref, wc_ref, g_ref, dp_scr, dqk_scr):
    pairs, seq, duo = q_ref.shape
    heads2 = dp_scr.shape[0]
    hp = pl.program_id(0)

    @pl.when(hp == 0)
    def _():
        for i in range(pairs):
            rows = jnp.dot(wc_ref[i], nt_ref[:, i * seq : (i + 1) * seq], preferred_element_type=F32)
            for j in range(heads2):
                dp_scr[j, i] = rows[2 * j : 2 * j + 2]

    low, high = half_masks(duo)

    def pair(i, carry):
        probs = p_ref[i].astype(F32)
        term = probs * dp_scr[hp, i][:, None, :]
        dlog = (term - probs * jnp.sum(term, axis=-1, keepdims=True)).astype(BF16)
        wide = jnp.concatenate([dlog[0], dlog[1]], axis=1)
        dq = jnp.dot(wide, stack_halves(k_ref[i], low, high), preferred_element_type=F32)
        dk = lax.dot_general(
            dlog.reshape(2 * seq, seq), stack_halves(q_ref[i], low, high), TN, preferred_element_type=F32
        )
        dqk_scr[i, :, :duo] = dq.astype(BF16)
        dqk_scr[i, :, duo:] = dk.astype(BF16)
        return carry

    lax.fori_loop(0, pairs, pair, 0, unroll=4)
    grad = jnp.dot(nt_ref[...], dqk_scr[...].reshape(pairs * seq, 2 * duo), preferred_element_type=F32)
    g_ref[0] = grad[:, :duo].astype(BF16)
    g_ref[1] = grad[:, duo:].astype(BF16)


def backward(normed_t, qk, probs, wc):
    pairs, heads, seq, _ = probs.shape
    width = normed_t.shape[0]
    duo = 2 * (width // heads)
    duos = heads // 2
    return pl.pallas_call(
        backward_kernel,
        grid=(duos,),
        in_specs=[
            pl.BlockSpec((width, pairs * seq), lambda h: (0, 0)),
            pl.BlockSpec((pairs, seq, duo), lambda h: (0, 0, h)),
            pl.BlockSpec((pairs, seq, duo), lambda h: (0, 0, duos + h)),
            pl.BlockSpec((pairs, 2, seq, seq), lambda h: (0, h, 0, 0)),
            pl.BlockSpec(wc.shape, lambda h: (0, 0, 0)),
        ],
        out_specs=pl.BlockSpec((2, width, duo), lambda h: (0, 0, h)),
        out_shape=jax.ShapeDtypeStruct((2, width, width), BF16),
        scratch_shapes=[pltpu.VMEM((duos, pairs, 2, seq), F32), pltpu.VMEM((pairs, seq, 2 * duo), BF16)],
        compiler_params=pltpu.CompilerParams(vmem_limit_bytes=VMEM_LIMIT),
        cost_estimate=pl.CostEstimate(flops=30_000_000_000, bytes_accessed=20_000_000, transcendentals=0),
        name="attend_backward",
    )(normed_t, qk, qk, probs, wc)


def shards(hidden, attn_weight, norm_gain, pos_bias, score_weight, pair_lengths, labels):
    q_local, c_local, seq, width = hidden.shape
    pairs = q_local * c_local
    heads = pos_bias.shape[0]
    head_size = width // heads
    wqk = lax.all_gather(attn_weight[:, : 2 * width], "dp", axis=0, tiled=True)
    wvo = lax.all_gather(attn_weight[:, 2 * width :], "dp", axis=0, tiled=True)
    wv, wo = wvo[:, :width], wvo[:, width:]
    pair_len = pair_lengths.reshape(pairs)
    len_col = pair_len.astype(F32).reshape(pairs, 1)
    gain = norm_gain.reshape(1, width)
    sw = score_weight.reshape(1, width)
    tokens = hidden.reshape(pairs, seq, width)
    normed_t, qk, probs, u, hsum = forward(tokens, pair_len, gain, wqk, pos_bias)
    params = pltpu.CompilerParams(vmem_limit_bytes=VMEM_LIMIT)
    ctx, pooled, score_col = pl.pallas_call(
        functools.partial(score_kernel, head_size),
        out_shape=[
            jax.ShapeDtypeStruct((pairs, width), BF16),
            jax.ShapeDtypeStruct((pairs, width), F32),
            jax.ShapeDtypeStruct((pairs, 1), F32),
        ],
        compiler_params=params,
        name="score_forward",
    )(u, wv, wo, hsum.reshape(pairs, width), len_col, sw)
    scores = score_col.reshape(q_local, c_local)
    mine = jnp.stack([scores, labels.astype(F32)])
    every = lax.all_gather(mine, "cand", axis=2, tiled=True)
    all_scores, all_target = every[0], jnp.exp(every[1])
    highest = jnp.max(all_scores, axis=1)
    expsum = jnp.sum(jnp.exp(all_scores - highest[:, None]), axis=1)
    target_sum = jnp.sum(all_target, axis=1)
    target_dot = jnp.sum(all_target * all_scores, axis=1)
    loss = highest + jnp.log(expsum) - target_dot / target_sum
    target = jnp.exp(labels.astype(F32))
    score_grad = jnp.exp(scores - highest[:, None]) / expsum[:, None] - target / target_sum[:, None]
    wc, gvo = pl.pallas_call(
        functools.partial(middle_kernel, head_size),
        out_shape=[
            jax.ShapeDtypeStruct(u.shape, BF16),
            jax.ShapeDtypeStruct((width, 2 * width), BF16),
        ],
        compiler_params=params,
        name="score_backward",
    )(score_grad.reshape(pairs, 1), pooled, len_col, sw, u, ctx, wv, wo)
    gvo = lax.psum_scatter(gvo, "dp", scatter_dimension=0, tiled=True)
    gqk = backward(normed_t, qk, probs, wc)
    gqk = lax.psum_scatter(gqk, "dp", scatter_dimension=1, tiled=True)
    shard = jnp.concatenate([gqk[0], gqk[1], gvo], axis=1)
    shard = lax.psum(shard, "cand").astype(F32)
    squares = lax.psum(jnp.sum(shard * shard), "dp")
    rms_value = jnp.sqrt(squares / (4.0 * width * width))
    update = shard / (rms_value + EPS)
    return (update, loss)


def solution(mesh):
    in_specs = (
        P("dp", "cand", None, None),
        P("dp", None),
        P(),
        P(),
        P(),
        P("dp", "cand"),
        P("dp", "cand"),
    )
    out_specs = (P("dp", None), P("dp"))
    return jax.shard_map(shards, mesh=mesh, in_specs=in_specs, out_specs=out_specs, check_vma=False)
```

time: 464 us -> 372 us (0.80)
  matrix products: 83.9 us -> 0 us
  local copies, waits for them, and re-layouts: 76.2 us -> 11.1 us
  Pallas kernels: 0 us -> 59.6 us
  waiting for transfers between devices: 204 us -> 251 us
  other arithmetic: 47.1 us -> 7.65 us
  blocking collectives: 34.2 us -> 27.1 us
    dot_general x11 -> x0, matrix products: 83.9 us -> none  [the longest x3 24.4 us: attend(): jnp.einsum('bhqk,bkhd->bqhd', probs, parts[:, :, 2], preferred_element_ty...]
    pallas_call x0 -> x4, Pallas kernels: none -> 59.6 us  [the longest x1 27.3 us: forward(): pl.pallas_call(functools.partial(forward_kernel, hpad), grid=(pairs // ba...]
    reduce_scatter x1 -> x2, waiting for transfers between devices: 94.1 us -> 139 us  [the longest x1 71.2 us: shards(): gvo = lax.psum_scatter(gvo, 'dp', scatter_dimension=0, tiled=True)]
    add_any x1 -> x0, local copies, waits for them, and re-layouts: 26.1 us -> none  [attend(): parts[:, :, 0]]
    reduce_sum x8 -> x2, other arithmetic: 24.8 us -> 0.26 us  [the longest x1 0.19 us: shards(): target_dot = jnp.sum(all_target * all_scores, axis=1)]
    unnamed x47 -> x9, local copies, waits for them, and re-layouts: 22.7 us -> 1.43 us
    convert_element_type x3 -> x1, local copies, waits for them, and re-layouts: 19.9 us -> 0.68 us  [shards(): len_col = pair_len.astype(F32).reshape(pairs, 1)]
    convert_element_type x5 -> x1, other arithmetic: 7.44 us -> 0.01 us  [shards(): len_col = pair_len.astype(F32).reshape(pairs, 1)]
  transfers between devices with their start and end apart: 3 -> 5, of which waited for: 3 -> 5; matrix products, arithmetic and copies ran while one was open for 2% -> 1% of each run, Pallas kernels for 0% -> 7%
where the time goes in v1:
time: 372 us; the launch traced here: 371 us
  waiting for transfers between devices  251 us (67%)
  Pallas kernels  59.6 us (16%)
  blocking collectives  27.1 us (7%)
  between operations  14.5 us (4%)
  local copies, waits for them, and re-layouts  11.1 us (3%)
  other arithmetic  7.65 us (2%)
    reduce_scatter x1, waiting for transfers between devices, shards(): gvo = lax.psum_scatter(gvo, 'dp', scatter_dimension=0, tiled=True)  71.2 us
    reduce_scatter x1, waiting for transfers between devices, shards(): gqk = lax.psum_scatter(gqk, 'dp', scatter_dimension=1, tiled=True)  67.7 us
    all_gather x1, waiting for transfers between devices, shards(): wqk = lax.all_gather(attn_weight[:, :2 * width], 'dp', axis=0, tiled=True)  52.3 us
    psum x1, waiting for transfers between devices, shards(): shard = lax.psum(shard, 'cand').astype(F32)  34 us
    pallas_call x1, Pallas kernels, forward(): pl.pallas_call(functools.partial(forward_kernel, hpad), grid=(pairs // ba...  27.3 us
    all_gather x1, waiting for transfers between devices, shards(): wvo = lax.all_gather(attn_weight[:, 2 * width:], 'dp', axis=0, tiled=True)  24.4 us
    pallas_call x1, Pallas kernels, backward(): pl.pallas_call(backward_kernel, grid=(duos,), in_specs=[pl.BlockSpec((wid...  24 us
    psum x1, blocking collectives, shards(): squares = lax.psum(jnp.sum(shard * shard), 'dp')  22 us
  transfers between devices with their start and end apart: 5, of which 5 were waited for; matrix products, arithmetic and copies ran while one was open for 1% of the time, Pallas kernels for 7%

profile of v1, /device:TPU:0, one launch (start us, length us, event | category | flops | bytes accessed | tf_op | source)
XLA Modules:
  0.0 371.1 jit_solution(17640775955058266685)
XLA Ops:
  7.2 0.0 copy-start.3
  7.2 0.0 copy-start
  7.2 0.0 copy-start.1
  7.2 0.0 copy-start.2
  7.2 0.0 all-gather.3.cloned.1.call-start
  7.3 1.9 fusion.6
  9.1 0.0 all-gather.3.cloned.1.call-update
  9.2 0.0 all-gather.5.cloned.1.call-start
  9.2 0.7 all-gather.5.cloned.1.call-update
  9.9 0.0 reduce-scatter.3.cloned.1.call-start
  10.0 0.0 copy-done.3
  10.0 0.6 reshape.41.len_ref
  10.6 0.6 reshape.45.sw_ref
  11.2 0.6 reshape.43.gain_ref
  11.8 0.7 convert_element_type.24.len_ref
  12.4 52.3 %all-gather.3.cloned.1.call-done.w_ref = bf16[768,1536]{1,0:T(8,128)(2,1)} async-done(((bf16[96,1536]{1,0:T(8,128)(2,1)}), bf16[768,1536]{1,0:T(8,128)(2,1)}) %all-gather.3.cloned.1.call-update) | async-done | bytes 2359312 | tf_op jit(solution)/shard_map/all_gather | solution.py:213
  64.8 27.3 %attend_forward.1 = (bf16[768,2048]{1,0:T(8,128)(2,1)}, bf16[16,128,1536]{2,1,0:T(8,128)(2,1)}, bf16[16,12,128,128]{3,2,1,0:T(8,128)(2,1)}, bf16[16,16,768]{2,1,0:T(8,128)(2,1)}, f32[16,1,768]{2,1,0:T(1,128)}) custom-call(s32[16]{0:T(128)} %reshape.41.len_ref, bf16[16,128,768]{2,1,0:T(8,128)(2,1)} %bitcast.22, f32[1,768]{1,0:T(1,128)} %reshape.43.gain_ref, ...), custom_call_target="tpu_custom_call" | custom-call | flops 30000001024 | bytes 24000000 | tf_op jit(solution)/shard_map/attend_forward/pallas_call | solution.py:78
  92.1 1.4 copy.23
  93.5 24.4 %all-gather.5.cloned.1.call-done = bf16[768,1536]{1,0:T(8,128)(2,1)} async-done(((bf16[96,1536]{1,0:T(8,128)(2,1)}), bf16[768,1536]{1,0:T(8,128)(2,1)}) %all-gather.5.cloned.1.call-update) | async-done | bytes 2359312 | tf_op jit(solution)/shard_map/all_gather | solution.py:214
  118.0 3.2 fusion.5
  121.2 3.3 score_forward.1
  124.4 0.8 reduce.2
  125.3 0.1 stack_reshape.3
  125.3 0.1 reshape.46
  125.4 0.1 copy.16
  125.5 5.2 %all_gather.11 = f32[2,2,32]{1,0,2:T(2,128)S(1)} all-gather(f32[2,2,8]{1,0,2:T(2,128)S(1)} %copy.16), channel_id=1, replica_groups=mesh['dp'=8,'cand'=4] {'cand'}, dimensions={2}, use_global_device_ids=true | all-gather | bytes 640 | tf_op jit(solution)/shard_map/all_gather | solution.py:235
  130.7 0.1 fusion.4
  130.8 0.1 copy.20
  130.8 0.1 copy.17
  130.9 0.2 fusion.1
  131.1 0.1 divide_subtract_fusion
  131.2 0.7 reshape.48.sg_ref
  131.9 4.9 %score_backward.1 = (bf16[16,16,768]{2,1,0:T(8,128)(2,1)}, bf16[768,1536]{1,0:T(8,128)(2,1)}) custom-call(f32[16,1]{1,0:T(8,128)} %reshape.48.sg_ref, f32[16,768]{1,0:T(8,128)} %get-tuple-element.18.pooled_ref, f32[16,1]{1,0:T(8,128)} %convert_element_type.24.len_ref, f32[1,768]{1,0:T(1,128)} %reshape.45.sw_ref, ...), custom_call_target="tpu_custom_call" | custom-call | tf_op jit(solution)/shard_map/score_backward/pallas_call | solution.py:244
  136.8 24.0 %attend_backward.1 = bf16[2,768,768]{2,1,0:T(8,128)(2,1)} custom-call(bf16[768,2048]{1,0:T(8,128)(2,1)} %get-tuple-element.12.nt_ref, bf16[16,128,1536]{2,1,0:T(8,128)(2,1)} %get-tuple-element.13.q_ref.k_ref, bf16[16,128,1536]{2,1,0:T(8,128)(2,1)} %get-tuple-element.13.q_ref.k_ref, bf16[16,12,128,128]{3,2,1,0:T(8,128)(2,1)} %get-tuple-element.14.p_ref, ...), custom_call_target="tpu_custom_call" | custom-call | flops 30000001024 | bytes 20000000 | tf_op jit(solution)/shard_map/attend_backward/pallas_call | solution.py:189
  160.9 0.0 reduce-scatter.3.cloned.1.call-update
  160.9 0.0 reduce-scatter.5.cloned.1.call-start
  160.9 0.5 reduce-scatter.5.cloned.1.call-update
  161.5 0.0 all-reduce.2.cloned.1.call-start
  161.5 67.7 %reduce-scatter.3.cloned.1.call-done = bf16[2,96,768]{2,1,0:T(8,128)(2,1)} async-done(((bf16[2,768,768]{2,1,0:T(8,128)(2,1)}), bf16[2,96,768]{2,1,0:T(8,128)(2,1)}) %reduce-scatter.3.cloned.1.call-update) | async-done | bytes 294928 | tf_op jit(solution)/shard_map/reduce_scatter | solution.py:255
  229.2 1.0 slice_bitcast_fusion.1
  230.2 71.2 %reduce-scatter.5.cloned.1.call-done = bf16[96,1536]{1,0:T(8,128)(2,1)} async-done(((bf16[768,1536]{1,0:T(8,128)(2,1)}), bf16[96,1536]{1,0:T(8,128)(2,1)}) %reduce-scatter.5.cloned.1.call-update) | async-done | bytes 294928 | tf_op jit(solution)/shard_map/reduce_scatter | solution.py:253
  301.4 1.8 pad_maximum_fusion
  303.2 0.0 all-reduce.2.cloned.1.call-update
  303.2 34.0 %all-reduce.2.cloned.1.call-done = bf16[96,3072]{1,0:T(8,128)(2,1)} async-done(((bf16[96,3072]{1,0:T(8,128)(2,1)}), bf16[96,3072]{1,0:T(8,128)(2,1)}) %all-reduce.2.cloned.1.call-update) | async-done | bytes 589840 | tf_op jit(solution)/shard_map/psum | solution.py:257
  337.2 2.0 fusion
  339.2 0.5 divide_subtract_fusion.1
  339.7 22.0 %psum.15 = f32[]{:T(128)} all-reduce(f32[]{:T(128)} %fusion), channel_id=1, replica_groups=mesh['dp'=8,'cand'=4] {'dp'}, use_global_device_ids=true, to_apply=%region_7.0 | all-reduce | flops 1 | bytes 8 | tf_op jit(solution)/shard_map/psum | solution.py:258
  362.4 2.2 convert_divide_fusion
  (6 shorter events, 0.0 us)
Async XLA Ops:
  7.2 2.8 copy-start.3
  7.2 3.4 copy-start
  7.2 4.0 %copy-start.1 = (f32[768]{0:T(1024)S(1)}, f32[768]{0:T(1024)}, u32[]{:S(2)}) copy-start(f32[768]{0:T(1024)} %param.9) | copy-start | bytes 9220
  7.2 5.2 %copy-start.2 = (s32[2,8]{1,0:T(2,128)S(1)}, s32[2,8]{1,0:T(2,128)}, u32[]{:S(2)}) copy-start(s32[2,8]{1,0:T(2,128)} %param.13) | copy-start | bytes 196
  7.2 57.6 %all-gather.3.cloned.1.call-start = ((), (), s32[]{:S(2)}) async-start(), calls=%async_computation.2 | async-start | bytes 2654208 | tf_op jit(solution)/shard_map/all_gather | solution.py:213
  9.2 108.8 %all-gather.5.cloned.1.call-start = ((), (), s32[]{:S(2)}) async-start(), calls=%async_computation.3 | async-start | bytes 2654208 | tf_op jit(solution)/shard_map/all_gather | solution.py:214
  9.9 219.3 %reduce-scatter.3.cloned.1.call-start = ((), (), s32[]{:S(2)}) async-start(), calls=%async_computation.4 | async-start | bytes 2654208 | tf_op jit(solution)/shard_map/reduce_scatter | solution.py:255
  160.9 140.5 %reduce-scatter.5.cloned.1.call-start = ((), (), s32[]{:S(2)}) async-start(), calls=%async_computation.5 | async-start | bytes 2654208 | tf_op jit(solution)/shard_map/reduce_scatter | solution.py:253
  161.5 175.8 %all-reduce.2.cloned.1.call-start = ((), (), s32[]{:S(2)}) async-start(), calls=%async_computation.6 | async-start | bytes 1179648 | tf_op jit(solution)/shard_map/psum | solution.py:257
Sparse Core Ops, SparseCore 0:
  10.2 54.5 all-gather.2
  67.5 50.3 all-gather.4
  161.0 68.1 reduce-scatter.2
  232.5 68.8 reduce-scatter.4
  304.2 33.0 all-reduce.1

commit v2 on v1

--- a/solution.py
+++ b/solution.py
@@ -35,8 +35,9 @@
     normed = (values * factor * gain_ref[...]).astype(BF16)
     norm_scr[...] = normed.reshape(batch, seq, width)
     nt_ref[...] = normed.T
-    qk = jnp.dot(normed, w_ref[...], preferred_element_type=F32)
-    qk_ref[...] = qk.astype(BF16).reshape(batch, seq, 2 * width)
+    for part in range(2):
+        proj = jnp.dot(normed, w_ref[part], preferred_element_type=F32)
+        qk_ref[:, :, part * width : (part + 1) * width] = proj.astype(BF16).reshape(batch, seq, width)
     low, high = half_masks(duo)
     col = lax.broadcasted_iota(jnp.int32, (1, seq), 1)
     row = lax.broadcasted_iota(jnp.int32, (seq, 1), 0)
@@ -69,7 +70,7 @@
     lax.fori_loop(0, batch, pair, 0)
 
 
-def forward(tokens, pair_len, gain, wqk, pos_bias):
+def forward(tokens, pair_len, gain, weights, pos_bias):
     pairs, seq, width = tokens.shape
     heads = pos_bias.shape[0]
     hpad = -(-heads // 16) * 16
@@ -82,7 +83,7 @@
             pl.BlockSpec(memory_space=pltpu.SMEM),
             pl.BlockSpec((batch, seq, width), lambda i: (i, 0, 0)),
             full(1, width),
-            full(width, 2 * width),
+            full(2, width, width),
             full(heads, seq, seq),
         ],
         out_specs=[
@@ -103,7 +104,7 @@
         compiler_params=pltpu.CompilerParams(vmem_limit_bytes=VMEM_LIMIT),
         cost_estimate=pl.CostEstimate(flops=30_000_000_000, bytes_accessed=24_000_000, transcendentals=0),
         name="attend_forward",
-    )(pair_len, tokens, gain, wqk, pos_bias)
+    )(pair_len, tokens, gain, weights, pos_bias)
 
 
 def head_mask(hpad, width, head_size):
@@ -113,9 +114,9 @@
     return ((lane >= start) & (lane < start + head_size)).astype(F32)
 
 
-def score_kernel(head_size, u_ref, wv_ref, wo_ref, hsum_ref, len_ref, sw_ref, ctx_ref, pooled_ref, score_ref):
+def score_kernel(head_size, u_ref, w_ref, hsum_ref, len_ref, sw_ref, ctx_ref, pooled_ref, score_ref):
     pairs, hpad, width = u_ref.shape
-    mixed = jnp.dot(u_ref[...].reshape(pairs * hpad, width), wv_ref[...], preferred_element_type=F32)
+    mixed = jnp.dot(u_ref[...].reshape(pairs * hpad, width), w_ref[0], preferred_element_type=F32)
     mask = head_mask(hpad, width, head_size)
     ctx = jnp.sum(mixed.reshape(pairs, hpad, width) * mask[None], axis=1)
     ctx_ref[...] = ctx.astype(BF16)
@@ -123,14 +124,14 @@
     mean = ctx * share
     high = mean.astype(BF16)
     low = (mean - high.astype(F32)).astype(BF16)
-    both = jnp.dot(jnp.concatenate([high, low], axis=0), wo_ref[...], preferred_element_type=F32)
+    both = jnp.dot(jnp.concatenate([high, low], axis=0), w_ref[1], preferred_element_type=F32)
     pooled = hsum_ref[...] * share + both[:pairs] + both[pairs:]
     pooled_ref[...] = pooled
     factor = lax.rsqrt(jnp.mean(pooled * pooled, axis=-1, keepdims=True) + EPS)
     score_ref[...] = jnp.sum(pooled * factor * sw_ref[...], axis=-1, keepdims=True)
 
 
-def middle_kernel(head_size, sg_ref, pooled_ref, len_ref, sw_ref, u_ref, ctx_ref, wv_ref, wo_ref, wc_ref, gvo_ref):
+def middle_kernel(head_size, sg_ref, pooled_ref, len_ref, sw_ref, u_ref, ctx_ref, w_ref, wc_ref, gvo_ref):
     pairs, hpad, width = u_ref.shape
     pooled = pooled_ref[...]
     sw = sw_ref[...]
@@ -138,17 +139,21 @@
     dot = jnp.sum(pooled * sw, axis=-1, keepdims=True) * (1.0 / width)
     grad = sg_ref[...] * (factor * sw - pooled * (factor * factor * factor * dot))
     out_grad = (grad / len_ref[...]).astype(BF16)
-    cg = lax.dot_general(out_grad, wo_ref[...], NT, preferred_element_type=F32).astype(BF16).astype(F32)
+    cg = lax.dot_general(out_grad, w_ref[1], NT, preferred_element_type=F32).astype(BF16).astype(F32)
     mask = head_mask(hpad, width, head_size)
     spread = (cg[:, None, :] * mask[None]).astype(BF16).reshape(pairs * hpad, width)
-    wc = lax.dot_general(spread, wv_ref[...], NT, preferred_element_type=F32)
+    wc = lax.dot_general(spread, w_ref[0], NT, preferred_element_type=F32)
     wc_ref[...] = wc.astype(BF16).reshape(pairs, hpad, width)
     u = u_ref[...].reshape(pairs * hpad, width)
-    gvo_ref[:, :width] = lax.dot_general(u, spread, TN, preferred_element_type=F32).astype(BF16)
-    gvo_ref[:, width:] = lax.dot_general(ctx_ref[...], out_grad, TN, preferred_element_type=F32).astype(BF16)
-
-
-def backward_kernel(nt_ref, q_ref, k_ref, p_ref, wc_ref, g_ref, dp_scr, dqk_scr):
+    _, duos, _, lanes = gvo_ref.shape
+    gv = lax.dot_general(u, spread, TN, preferred_element_type=F32).astype(BF16)
+    go = lax.dot_general(ctx_ref[...], out_grad, TN, preferred_element_type=F32).astype(BF16)
+    for j in range(duos):
+        gvo_ref[0, j] = gv[:, j * lanes : (j + 1) * lanes]
+        gvo_ref[1, j] = go[:, j * lanes : (j + 1) * lanes]
+
+
+def backward_kernel(nt_ref, q_ref, k_ref, p_ref, wc_ref, gin_ref, g_ref, dp_scr, dqk_scr):
     pairs, seq, duo = q_ref.shape
     heads2 = dp_scr.shape[0]
     hp = pl.program_id(0)
@@ -177,11 +182,11 @@
 
     lax.fori_loop(0, pairs, pair, 0, unroll=4)
     grad = jnp.dot(nt_ref[...], dqk_scr[...].reshape(pairs * seq, 2 * duo), preferred_element_type=F32)
-    g_ref[0] = grad[:, :duo].astype(BF16)
-    g_ref[1] = grad[:, duo:].astype(BF16)
-
-
-def backward(normed_t, qk, probs, wc):
+    g_ref[0, 0] = grad[:, :duo].astype(BF16)
+    g_ref[1, 0] = grad[:, duo:].astype(BF16)
+
+
+def backward(normed_t, qk, probs, wc, grads):
     pairs, heads, seq, _ = probs.shape
     width = normed_t.shape[0]
     duo = 2 * (width // heads)
@@ -195,14 +200,236 @@
             pl.BlockSpec((pairs, seq, duo), lambda h: (0, 0, duos + h)),
             pl.BlockSpec((pairs, 2, seq, seq), lambda h: (0, h, 0, 0)),
             pl.BlockSpec(wc.shape, lambda h: (0, 0, 0)),
-        ],
-        out_specs=pl.BlockSpec((2, width, duo), lambda h: (0, 0, h)),
-        out_shape=jax.ShapeDtypeStruct((2, width, width), BF16),
+            pl.BlockSpec(memory_space=pl.ANY),
+        ],
+        out_specs=pl.BlockSpec((2, 1, width, duo), lambda h: (0, h, 0, 0)),
+        out_shape=jax.ShapeDtypeStruct(grads.shape, BF16),
+        input_output_aliases={5: 0},
         scratch_shapes=[pltpu.VMEM((duos, pairs, 2, seq), F32), pltpu.VMEM((pairs, seq, 2 * duo), BF16)],
         compiler_params=pltpu.CompilerParams(vmem_limit_bytes=VMEM_LIMIT),
         cost_estimate=pl.CostEstimate(flops=30_000_000_000, bytes_accessed=20_000_000, transcendentals=0),
         name="attend_backward",
-    )(normed_t, qk, qk, probs, wc)
+    )(normed_t, qk, qk, probs, wc, grads)
+
+
+MESH = pl.DeviceIdType.MESH
+
+
+def greet(targets):
+    barrier = pltpu.get_barrier_semaphore()
+    for target in targets:
+        pl.semaphore_signal(barrier, inc=1, device_id=target, device_id_type=MESH)
+    pl.semaphore_wait(barrier, len(targets))
+
+
+def push(src, dst, send, recv, target):
+    copy = pltpu.make_async_remote_copy(
+        src_ref=src, dst_ref=dst, send_sem=send, recv_sem=recv, device_id=target, device_id_type=MESH
+    )
+    copy.start()
+    return copy
+
+
+def gather_kernel(n, m, x_ref, o_ref, own_sem, z_send, x_send, y_send, c_send, recv):
+    rows = x_ref.shape[0]
+    wide = x_ref.shape[1] // m
+    half, duo = n // 2, m // 2
+    d, c = lax.axis_index("dp"), lax.axis_index("cand")
+    z, x = d // 2, d % 2
+    y, core = c // 2, c % 2
+    across = (d + 1 - 2 * x, c)
+    other = (d, c + 1 - 2 * core)
+    zs = [(2 * lax.rem(z + j, half) + x, c) for j in range(1, half)]
+    ys = [(d, 2 * lax.rem(y + j, duo) + core) for j in range(1, duo)]
+    greet(zs + ys + [across, other])
+    mine = x_ref.at[:, pl.ds(pl.multiple_of(c * wide, 128), wide)]
+    copies = []
+    for j in range(half - 1):
+        copies.append(push(mine, o_ref.at[c, d], z_send.at[j], recv.at[c, d], zs[j]))
+    copies.append(push(mine, o_ref.at[c, d], x_send.at[0], recv.at[c, d], across))
+    local = []
+    for k in range(m):
+        local.append(
+            pltpu.make_async_copy(x_ref.at[:, k * wide : (k + 1) * wide], o_ref.at[k, d], own_sem.at[k])
+        )
+        local[-1].start()
+
+    def arrived(piece, block):
+        ref = o_ref.at[piece, block]
+        pltpu.make_async_copy(ref, ref, recv.at[piece, block]).wait()
+
+    def spread(block, slot):
+        ref = o_ref.at[c, block]
+        for j in range(duo - 1):
+            copies.append(push(ref, ref, y_send.at[slot, j], recv.at[c, block], ys[j]))
+        copies.append(push(ref, ref, c_send.at[0, slot], recv.at[c, block], other))
+
+    for j in range(1, half):
+        block = 2 * lax.rem(z - j + half, half) + x
+        arrived(c, block)
+        ref = o_ref.at[c, block]
+        copies.append(push(ref, ref, x_send.at[j], recv.at[c, block], across))
+        spread(block, j - 1)
+    far = []
+    for j in range(half):
+        block = 2 * lax.rem(z - j + half, half) + 1 - x
+        arrived(c, block)
+        spread(block, half - 1 + j)
+    order = [2 * lax.rem(z - j + half, half) + x for j in range(1, half)]
+    order += [2 * lax.rem(z - j + half, half) + 1 - x for j in range(half)]
+    for slot, block in enumerate(order):
+        for j in range(1, duo):
+            piece = 2 * lax.rem(y - j + duo, duo) + core
+            arrived(piece, block)
+            ref = o_ref.at[piece, block]
+            copies.append(push(ref, ref, c_send.at[j, slot], recv.at[piece, block], other))
+    for slot, block in enumerate(order):
+        for j in range(duo):
+            arrived(2 * lax.rem(y - j + duo, duo) + 1 - core, block)
+    for copy in local:
+        copy.wait()
+    for copy in copies:
+        copy.wait_send()
+
+
+def gather_weights(block, n, m):
+    rows, total = block.shape
+    dma = pltpu.SemaphoreType.DMA
+    return pl.pallas_call(
+        functools.partial(gather_kernel, n, m),
+        in_specs=[pl.BlockSpec(memory_space=pltpu.VMEM)],
+        out_specs=pl.BlockSpec(memory_space=pltpu.VMEM),
+        out_shape=jax.ShapeDtypeStruct((m, n, rows, total // m), block.dtype),
+        scratch_shapes=[
+            dma((m,)), dma((n // 2,)), dma((n // 2,)), dma((n, max(m // 2 - 1, 1))), dma((m // 2, n)), dma((m, n))
+        ],
+        compiler_params=pltpu.CompilerParams(
+            collective_id=0, has_side_effects=True, vmem_limit_bytes=VMEM_LIMIT
+        ),
+        name="gather_weights",
+    )(block)
+
+
+def reduce_kernel(n, m, g_ref, o_ref, r1, s1, r2, s2, r3, s3, r4, fin, sq, r6,
+                  t1, v1, t2, v2, t3, v3, t4, v4, t5, v5, t6, v6):
+    chunks, duo, _, half, _, rows, lanes = g_ref.shape
+    d, c = lax.axis_index("dp"), lax.axis_index("cand")
+    z, x = d // 2, d % 2
+    y, core = c // 2, c % 2
+    across = (d + 1 - 2 * x, c)
+    other = (d, c + 1 - 2 * core)
+    cands = [(d, lax.rem(c + j, m)) for j in range(1, m)]
+    dps = [(lax.rem(d + j, n), c) for j in range(1, n)]
+    greet(cands + dps)
+    copies = []
+
+    def send(*args):
+        copies.append(push(*args))
+
+    def arrived(ref, sem):
+        pltpu.make_async_copy(ref, ref, sem).wait()
+
+    for k in range(chunks):
+        send(g_ref.at[k, :, 1 - core], r1.at[k], t1.at[k], v1.at[k], other)
+
+    def stage_y(k):
+        arrived(r1.at[k], v1.at[k])
+        s1[k] = (g_ref[k, :, core].astype(F32) + r1[k].astype(F32)).astype(BF16)
+        for j in range(1, duo):
+            peer = lax.rem(y + j, duo)
+            send(s1.at[k, peer], r2.at[k, j - 1], t2.at[k, j - 1], v2.at[k, j - 1], (d, 2 * peer + core))
+
+    def stage_x(k):
+        total = s1[k, y].astype(F32)
+        for j in range(1, duo):
+            arrived(r2.at[k, j - 1], v2.at[k, j - 1])
+            total = total + r2[k, j - 1].astype(F32)
+        s2[k] = total.astype(BF16)
+        send(s2.at[k, :, 1 - x], r3.at[k], t3.at[k], v3.at[k], across)
+
+    def stage_z(k):
+        arrived(r3.at[k], v3.at[k])
+        s3[k] = (s2[k, :, x].astype(F32) + r3[k].astype(F32)).astype(BF16)
+        for j in range(1, half):
+            peer = lax.rem(z + j, half)
+            send(s3.at[k, peer], r4.at[k, j - 1], t4.at[k, j - 1], v4.at[k, j - 1], (2 * peer + x, c))
+
+    def stage_cand(k):
+        total = s3[k, z].astype(F32)
+        for j in range(1, half):
+            arrived(r4.at[k, j - 1], v4.at[k, j - 1])
+            total = total + r4[k, j - 1].astype(F32)
+        fin[k, c] = total.astype(BF16)
+        for j in range(1, m):
+            send(fin.at[k, c], fin.at[k, c], t5.at[k, j - 1], v5.at[k, j - 1], cands[j - 1])
+
+    stages = (stage_x, stage_z, stage_cand)
+    for k in range(chunks):
+        stage_y(k)
+    for t in range(chunks + 2):
+        for lag, stage in enumerate(stages):
+            if 0 <= t - lag < chunks:
+                stage(t - lag)
+    for k in range(chunks):
+        for j in range(1, m):
+            arrived(fin.at[k, lax.rem(c - j + m, m)], v5.at[k, j - 1])
+    part = jnp.zeros((8, lanes), F32)
+    for k in range(chunks):
+        block = fin[k].astype(F32).reshape(m * rows // 8, 8, lanes)
+        part = part + jnp.sum(block * block, axis=0)
+    sq[...] = part
+    r6[d] = part
+    for j in range(1, n):
+        send(sq, r6.at[d], t6.at[j - 1], v6.at[j - 1], dps[j - 1])
+    for j in range(1, n):
+        arrived(r6.at[lax.rem(d - j + n, n)], v6.at[j - 1])
+    count = chunks * m * lanes * n * rows
+    squares = jnp.sum(jnp.sum(jnp.sum(r6[...], axis=0), axis=0, keepdims=True), axis=1, keepdims=True)
+    scale = 1.0 / (jnp.sqrt(squares / count) + EPS)
+    for k in range(chunks):
+        for i in range(m):
+            at = (k * m + i) * lanes
+            o_ref[:, at : at + lanes] = fin[k, i].astype(F32) * scale
+    for copy in copies:
+        copy.wait_send()
+
+
+def reduce_update(grads, n, m):
+    blocks, width, lanes = grads.shape
+    rows = width // n
+    duo, half = m // 2, n // 2
+    chunks = blocks // m
+    dma = pltpu.SemaphoreType.DMA
+    vmem = pltpu.VMEM
+    near, far = max(duo - 1, 1), max(half - 1, 1)
+    return pl.pallas_call(
+        functools.partial(reduce_kernel, n, m),
+        in_specs=[pl.BlockSpec(memory_space=pltpu.VMEM)],
+        out_specs=pl.BlockSpec(memory_space=pltpu.VMEM),
+        out_shape=jax.ShapeDtypeStruct((rows, blocks * lanes), F32),
+        scratch_shapes=[
+            vmem((chunks, duo, half, 2, rows, lanes), BF16),
+            vmem((chunks, duo, half, 2, rows, lanes), BF16),
+            vmem((chunks, near, half, 2, rows, lanes), BF16),
+            vmem((chunks, half, 2, rows, lanes), BF16),
+            vmem((chunks, half, rows, lanes), BF16),
+            vmem((chunks, half, rows, lanes), BF16),
+            vmem((chunks, far, rows, lanes), BF16),
+            vmem((chunks, m, rows, lanes), BF16),
+            vmem((8, lanes), F32),
+            vmem((n, 8, lanes), F32),
+            dma((chunks,)), dma((chunks,)),
+            dma((chunks, near)), dma((chunks, near)),
+            dma((chunks,)), dma((chunks,)),
+            dma((chunks, far)), dma((chunks, far)),
+            dma((chunks, m - 1)), dma((chunks, m - 1)),
+            dma((n - 1,)), dma((n - 1,)),
+        ],
+        compiler_params=pltpu.CompilerParams(
+            collective_id=1, has_side_effects=True, vmem_limit_bytes=VMEM_LIMIT
+        ),
+        name="reduce_update",
+    )(grads.reshape(chunks, duo, 2, half, 2, rows, lanes))
 
 
 def shards(hidden, attn_weight, norm_gain, pos_bias, score_weight, pair_lengths, labels):
@@ -210,18 +437,24 @@
     pairs = q_local * c_local
     heads = pos_bias.shape[0]
     head_size = width // heads
-    wqk = lax.all_gather(attn_weight[:, : 2 * width], "dp", axis=0, tiled=True)
-    wvo = lax.all_gather(attn_weight[:, 2 * width :], "dp", axis=0, tiled=True)
-    wv, wo = wvo[:, :width], wvo[:, width:]
+    n, m = lax.axis_size("dp"), lax.axis_size("cand")
+    weights = gather_weights(attn_weight, n, m).reshape(4, m // 4, width, 4 * width // m)
+    weights = weights.transpose(0, 2, 1, 3).reshape(4, width, width)
     pair_len = pair_lengths.reshape(pairs)
     len_col = pair_len.astype(F32).reshape(pairs, 1)
     gain = norm_gain.reshape(1, width)
     sw = score_weight.reshape(1, width)
     tokens = hidden.reshape(pairs, seq, width)
-    normed_t, qk, probs, u, hsum = forward(tokens, pair_len, gain, wqk, pos_bias)
+    normed_t, qk, probs, u, hsum = forward(tokens, pair_len, gain, weights, pos_bias)
     params = pltpu.CompilerParams(vmem_limit_bytes=VMEM_LIMIT)
+    whole = lambda *shape: pl.BlockSpec(shape, lambda i: (0,) * len(shape))
+    w_spec = pl.BlockSpec((2, width, width), lambda i: (1, 0, 0))
+    col, wide = whole(pairs, 1), whole(pairs, width)
     ctx, pooled, score_col = pl.pallas_call(
         functools.partial(score_kernel, head_size),
+        grid=(1,),
+        in_specs=[whole(*u.shape), w_spec, wide, col, whole(1, width)],
+        out_specs=[wide, wide, col],
         out_shape=[
             jax.ShapeDtypeStruct((pairs, width), BF16),
             jax.ShapeDtypeStruct((pairs, width), F32),
@@ -229,7 +462,7 @@
         ],
         compiler_params=params,
         name="score_forward",
-    )(u, wv, wo, hsum.reshape(pairs, width), len_col, sw)
+    )(u, weights, hsum.reshape(pairs, width), len_col, sw)
     scores = score_col.reshape(q_local, c_local)
     mine = jnp.stack([scores, labels.astype(F32)])
     every = lax.all_gather(mine, "cand", axis=2, tiled=True)
@@ -241,23 +474,21 @@
     loss = highest + jnp.log(expsum) - target_dot / target_sum
     target = jnp.exp(labels.astype(F32))
     score_grad = jnp.exp(scores - highest[:, None]) / expsum[:, None] - target / target_sum[:, None]
-    wc, gvo = pl.pallas_call(
+    duos, duo = heads // 2, 2 * head_size
+    wc, grads = pl.pallas_call(
         functools.partial(middle_kernel, head_size),
+        grid=(1,),
+        in_specs=[col, wide, col, whole(1, width), whole(*u.shape), wide, w_spec],
+        out_specs=[whole(*u.shape), pl.BlockSpec((2, duos, width, duo), lambda i: (1, 0, 0, 0))],
         out_shape=[
             jax.ShapeDtypeStruct(u.shape, BF16),
-            jax.ShapeDtypeStruct((width, 2 * width), BF16),
+            jax.ShapeDtypeStruct((4, duos, width, duo), BF16),
         ],
         compiler_params=params,
         name="score_backward",
-    )(score_grad.reshape(pairs, 1), pooled, len_col, sw, u, ctx, wv, wo)
-    gvo = lax.psum_scatter(gvo, "dp", scatter_dimension=0, tiled=True)
-    gqk = backward(normed_t, qk, probs, wc)
-    gqk = lax.psum_scatter(gqk, "dp", scatter_dimension=1, tiled=True)
-    shard = jnp.concatenate([gqk[0], gqk[1], gvo], axis=1)
-    shard = lax.psum(shard, "cand").astype(F32)
-    squares = lax.psum(jnp.sum(shard * shard), "dp")
-    rms_value = jnp.sqrt(squares / (4.0 * width * width))
-    update = shard / (rms_value + EPS)
+    )(score_grad.reshape(pairs, 1), pooled, len_col, sw, u, ctx, weights)
+    grads = backward(normed_t, qk, probs, wc, grads)
+    update = reduce_update(grads.reshape(4 * duos, width, duo), n, m)
     return (update, loss)
 
 

time: 372 us -> 174 us (0.47)
  waiting for transfers between devices: 251 us -> 0 us
  Pallas kernels: 59.6 us -> 156 us
  blocking collectives: 27.1 us -> 5.17 us
  between operations: 14.5 us -> 0.67 us
  other arithmetic: 7.65 us -> 3.04 us
    reduce_scatter x2 -> x0, waiting for transfers between devices: 139 us -> none  [the longest x1 71.2 us: shards(): gvo = lax.psum_scatter(gvo, 'dp', scatter_dimension=0, tiled=True)]
    pallas_call x2 -> x4, Pallas kernels: 8.23 us -> 104 us  [the longest x1 55 us: reduce_update(): pl.pallas_call(functools.partial(reduce_kernel, n, m), in_specs=[pl.Block...]
    all_gather x2 -> x0, waiting for transfers between devices: 76.8 us -> none  [the longest x1 52.3 us: shards(): wqk = lax.all_gather(attn_weight[:, :2 * width], 'dp', axis=0, tiled=True)]
    psum x1 -> x0, waiting for transfers between devices: 34 us -> none  [shards(): shard = lax.psum(shard, 'cand').astype(F32)]
    psum x1 -> x0, blocking collectives: 22 us -> none  [shards(): squares = lax.psum(jnp.sum(shard * shard), 'dp')]
    slice x2 -> x0, local copies, waits for them, and re-layouts: 5.09 us -> none  [the longest x1 3.2 us: shards(): wv, wo = (wvo[:, :width], wvo[:, width:])]
  transfers between devices with their start and end apart: 5 -> 0, of which waited for: 5 -> 0; matrix products, arithmetic and copies ran while one was open for 1% -> 0% of each run, Pallas kernels for 7% -> 0%
where the time goes in v2:
time: 174 us
  Pallas kernels  156 us (90%)
  local copies, waits for them, and re-layouts  9.38 us (5%)
  blocking collectives  5.17 us (3%)
  other arithmetic  3.04 us (2%)
    pallas_call x1, Pallas kernels, reduce_update(): pl.pallas_call(functools.partial(reduce_kernel, n, m), in_specs=[pl.Block...  55 us
    pallas_call x1, Pallas kernels, gather_weights(): pl.pallas_call(functools.partial(gather_kernel, n, m), in_specs=[pl.Block...  40.8 us
    pallas_call x1, Pallas kernels, forward(): pl.pallas_call(functools.partial(forward_kernel, hpad), grid=(pairs // ba...  27.4 us
    pallas_call x1, Pallas kernels, backward(): pl.pallas_call(backward_kernel, grid=(duos,), in_specs=[pl.BlockSpec((wid...  24.1 us
    all_gather x1, blocking collectives, shards(): every = lax.all_gather(mine, 'cand', axis=2, tiled=True)  5.17 us
    pallas_call x1, Pallas kernels, shards(): pl.pallas_call(functools.partial(middle_kernel, head_size), grid=(1,), in...  5.06 us
    unnamed x4, local copies, waits for them, and re-layouts  3.79 us

profile of v2, /device:TPU:0, one launch (start us, length us, event | category | flops | bytes accessed | tf_op | source)
XLA Modules:
  0.0 173.8 jit_solution(626065026297393778)
XLA Ops:
  0.6 1.3 reshape.41.len_ref
  1.9 0.7 convert_element_type.17
  2.6 0.7 convert_bitcast_fusion
  3.3 1.3 reshape.45.sw_ref
  4.5 1.3 reshape.43.gain_ref
  5.8 0.7 convert_element_type.20.len_ref
  6.5 40.8 %gather_weights.1 = bf16[4,8,96,768]{3,2,1,0:T(8,128)(2,1)} custom-call(bf16[96,3072]{1,0:T(8,128)(2,1)} %x_ref.1), custom_call_target="tpu_custom_call" | custom-call | tf_op jit(solution)/shard_map/gather_weights/pallas_call | solution.py:298
  47.3 27.4 %attend_forward.1 = (bf16[768,2048]{1,0:T(8,128)(2,1)}, bf16[16,128,1536]{2,1,0:T(8,128)(2,1)}, bf16[16,12,128,128]{3,2,1,0:T(8,128)(2,1)}, bf16[16,16,768]{2,1,0:T(8,128)(2,1)}, f32[16,1,768]{2,1,0:T(1,128)}) custom-call(s32[16]{0:T(128)} %reshape.41.len_ref, bf16[16,128,768]{2,1,0:T(8,128)(2,1)} %bitcast.24, f32[1,768]{1,0:T(1,128)} %reshape.43.gain_ref, ...), custom_call_target="tpu_custom_call" | custom-call | flops 30000001024 | bytes 24000000 | tf_op jit(solution)/shard_map/attend_forward/pallas_call | solution.py:79
  74.6 0.0 copy-start
  74.6 1.4 copy.24
  76.1 3.3 %score_forward.1 = (bf16[16,768]{1,0:T(8,128)(2,1)}, f32[16,768]{1,0:T(8,128)}, f32[16,1]{1,0:T(8,128)}) custom-call(bf16[16,16,768]{2,1,0:T(8,128)(2,1)} %get-tuple-element.15.u_ref, bf16[4,768,768]{2,1,0:T(8,128)(2,1)} %bitcast.20, f32[16,768]{1,0:T(8,128)} %bitcast.23, f32[16,1]{1,0:T(8,128)} %convert_element_type.20.len_ref, f32[1,768]{1,0:T(1,128)} %reshape.45.sw_ref), custom_call_target="tpu_custom_call" | custom-call | tf_op jit(solution)/shard_map/score_forward/pallas_call | solution.py:453
  79.3 0.8 reduce.2
  80.1 0.1 stack_reshape.3
  80.2 0.1 reshape.46
  80.3 0.1 copy.17
  80.4 5.2 %all_gather.3 = f32[2,2,32]{1,0,2:T(2,128)S(1)} all-gather(f32[2,2,8]{1,0,2:T(2,128)S(1)} %copy.17), channel_id=1, replica_groups=mesh['dp'=8,'cand'=4] {'cand'}, dimensions={2}, use_global_device_ids=true | all-gather | bytes 640 | tf_op jit(solution)/shard_map/all_gather | solution.py:468
  85.6 0.1 fusion.3
  85.7 0.1 copy.21
  85.7 0.1 copy.18
  85.8 0.2 fusion
  86.0 0.5 divide_subtract_fusion.1
  86.5 0.0 copy-done
  86.5 0.1 divide_subtract_fusion
  86.6 0.7 reshape.48.sg_ref
  87.3 5.1 %score_backward.1 = (bf16[16,16,768]{2,1,0:T(8,128)(2,1)}, bf16[4,6,768,128]{3,2,1,0:T(8,128)(2,1)}) custom-call(f32[16,1]{1,0:T(8,128)} %reshape.48.sg_ref, f32[16,768]{1,0:T(8,128)} %get-tuple-element.18.pooled_ref, f32[16,1]{1,0:T(8,128)} %convert_element_type.20.len_ref, f32[1,768]{1,0:T(1,128)} %reshape.45.sw_ref, ...), custom_call_target="tpu_custom_call" | custom-call | tf_op jit(solution)/shard_map/score_backward/pallas_call | solution.py:478
  92.3 24.1 %attend_backward.1 = bf16[4,6,768,128]{3,2,1,0:T(8,128)(2,1)} custom-call(bf16[768,2048]{1,0:T(8,128)(2,1)} %get-tuple-element.12.nt_ref, bf16[16,128,1536]{2,1,0:T(8,128)(2,1)} %get-tuple-element.13.q_ref.k_ref, bf16[16,128,1536]{2,1,0:T(8,128)(2,1)} %get-tuple-element.13.q_ref.k_ref, ...), custom_call_target="tpu_custom_call", output_to_operand_aliasing={{}: (5, {})} | custom-call | flops 30000001024 | bytes 20000000 | tf_op jit(solution)/shard_map/attend_backward/pallas_call | solution.py:194
  116.4 55.0 %reduce_update.1 = f32[96,3072]{1,0:T(8,128)} custom-call(bf16[6,2,2,4,2,96,128]{6,5,4,3,2,1,0:T(8,128)(2,1)} %bitcast.22), custom_call_target="tpu_custom_call" | custom-call | tf_op jit(solution)/shard_map/reduce_update/pallas_call | solution.py:405
  171.5 2.4 %copy.27 = f32[96,3072]{1,0:T(8,128)} copy(f32[96,3072]{1,0:T(8,128)} %reduce_update.1) | data formatting | bytes 2359296
  (1 shorter events, 0.0 us)
Async XLA Ops:
  74.6 11.9 %copy-start = (s32[2,8]{1,0:T(2,128)S(1)}, s32[2,8]{1,0:T(2,128)}, u32[]{:S(2)}) copy-start(s32[2,8]{1,0:T(2,128)} %param.13) | copy-start | bytes 196

commit v3 on v2

--- a/solution.py
+++ b/solution.py
@@ -151,65 +151,6 @@
     for j in range(duos):
         gvo_ref[0, j] = gv[:, j * lanes : (j + 1) * lanes]
         gvo_ref[1, j] = go[:, j * lanes : (j + 1) * lanes]
-
-
-def backward_kernel(nt_ref, q_ref, k_ref, p_ref, wc_ref, gin_ref, g_ref, dp_scr, dqk_scr):
-    pairs, seq, duo = q_ref.shape
-    heads2 = dp_scr.shape[0]
-    hp = pl.program_id(0)
-
-    @pl.when(hp == 0)
-    def _():
-        for i in range(pairs):
-            rows = jnp.dot(wc_ref[i], nt_ref[:, i * seq : (i + 1) * seq], preferred_element_type=F32)
-            for j in range(heads2):
-                dp_scr[j, i] = rows[2 * j : 2 * j + 2]
-
-    low, high = half_masks(duo)
-
-    def pair(i, carry):
-        probs = p_ref[i].astype(F32)
-        term = probs * dp_scr[hp, i][:, None, :]
-        dlog = (term - probs * jnp.sum(term, axis=-1, keepdims=True)).astype(BF16)
-        wide = jnp.concatenate([dlog[0], dlog[1]], axis=1)
-        dq = jnp.dot(wide, stack_halves(k_ref[i], low, high), preferred_element_type=F32)
-        dk = lax.dot_general(
-            dlog.reshape(2 * seq, seq), stack_halves(q_ref[i], low, high), TN, preferred_element_type=F32
-        )
-        dqk_scr[i, :, :duo] = dq.astype(BF16)
-        dqk_scr[i, :, duo:] = dk.astype(BF16)
-        return carry
-
-    lax.fori_loop(0, pairs, pair, 0, unroll=4)
-    grad = jnp.dot(nt_ref[...], dqk_scr[...].reshape(pairs * seq, 2 * duo), preferred_element_type=F32)
-    g_ref[0, 0] = grad[:, :duo].astype(BF16)
-    g_ref[1, 0] = grad[:, duo:].astype(BF16)
-
-
-def backward(normed_t, qk, probs, wc, grads):
-    pairs, heads, seq, _ = probs.shape
-    width = normed_t.shape[0]
-    duo = 2 * (width // heads)
-    duos = heads // 2
-    return pl.pallas_call(
-        backward_kernel,
-        grid=(duos,),
-        in_specs=[
-            pl.BlockSpec((width, pairs * seq), lambda h: (0, 0)),
-            pl.BlockSpec((pairs, seq, duo), lambda h: (0, 0, h)),
-            pl.BlockSpec((pairs, seq, duo), lambda h: (0, 0, duos + h)),
-            pl.BlockSpec((pairs, 2, seq, seq), lambda h: (0, h, 0, 0)),
-            pl.BlockSpec(wc.shape, lambda h: (0, 0, 0)),
-            pl.BlockSpec(memory_space=pl.ANY),
-        ],
-        out_specs=pl.BlockSpec((2, 1, width, duo), lambda h: (0, h, 0, 0)),
-        out_shape=jax.ShapeDtypeStruct(grads.shape, BF16),
-        input_output_aliases={5: 0},
-        scratch_shapes=[pltpu.VMEM((duos, pairs, 2, seq), F32), pltpu.VMEM((pairs, seq, 2 * duo), BF16)],
-        compiler_params=pltpu.CompilerParams(vmem_limit_bytes=VMEM_LIMIT),
-        cost_estimate=pl.CostEstimate(flops=30_000_000_000, bytes_accessed=20_000_000, transcendentals=0),
-        name="attend_backward",
-    )(normed_t, qk, qk, probs, wc, grads)
 
 
 MESH = pl.DeviceIdType.MESH
@@ -310,34 +251,44 @@
     )(block)
 
 
-def reduce_kernel(n, m, g_ref, o_ref, r1, s1, r2, s2, r3, s3, r4, fin, sq, r6,
-                  t1, v1, t2, v2, t3, v3, t4, v4, t5, v5, t6, v6):
-    chunks, duo, _, half, _, rows, lanes = g_ref.shape
+def stage_slots(duos, blocks, m):
+    plan = []
+    x_slot = -1
+    for k in range(blocks // m):
+        late = (k + 1) * m - 2 * duos
+        first = 0 if late <= 0 else 3 * (-(-late // 2) - 1) + 2
+        y_slot = first if first == 0 else first + 2
+        x_slot = max(y_slot + 1, x_slot) + 3
+        for stage, slot in enumerate((first, y_slot, x_slot, x_slot + 3, x_slot + 6)):
+            plan.append((slot, stage, k))
+    return sorted(plan)
+
+
+def backward_kernel(n, m, nt_ref, q_ref, k_ref, p_ref, wc_ref, gvo_ref, o_ref, dp_scr, dqk_scr, grads,
+                    r1, s1, r2, s2, r3, s3, r4, fin, sq, r6, own,
+                    t1, v1, t2, v2, t3, v3, t4, v4, t5, v5, t6, v6):
+    pairs, seq, span = q_ref.shape
+    duos = dp_scr.shape[0]
+    hp = pl.program_id(0)
+    chunks, duo, half, _, rows, lanes = r1.shape
     d, c = lax.axis_index("dp"), lax.axis_index("cand")
     z, x = d // 2, d % 2
     y, core = c // 2, c % 2
     across = (d + 1 - 2 * x, c)
     other = (d, c + 1 - 2 * core)
-    cands = [(d, lax.rem(c + j, m)) for j in range(1, m)]
-    dps = [(lax.rem(d + j, n), c) for j in range(1, n)]
-    greet(cands + dps)
-    copies = []
-
-    def send(*args):
-        copies.append(push(*args))
 
     def arrived(ref, sem):
         pltpu.make_async_copy(ref, ref, sem).wait()
 
-    for k in range(chunks):
-        send(g_ref.at[k, :, 1 - core], r1.at[k], t1.at[k], v1.at[k], other)
+    def stage_core(k):
+        push(grads.at[k * duo : (k + 1) * duo, 1 - core], r1.at[k], t1.at[k], v1.at[k], other)
 
     def stage_y(k):
         arrived(r1.at[k], v1.at[k])
-        s1[k] = (g_ref[k, :, core].astype(F32) + r1[k].astype(F32)).astype(BF16)
+        s1[k] = (grads[k * duo : (k + 1) * duo, core].astype(F32) + r1[k].astype(F32)).astype(BF16)
         for j in range(1, duo):
             peer = lax.rem(y + j, duo)
-            send(s1.at[k, peer], r2.at[k, j - 1], t2.at[k, j - 1], v2.at[k, j - 1], (d, 2 * peer + core))
+            push(s1.at[k, peer], r2.at[k, j - 1], t2.at[k, j - 1], v2.at[k, j - 1], (d, 2 * peer + core))
 
     def stage_x(k):
         total = s1[k, y].astype(F32)
@@ -345,14 +296,14 @@
             arrived(r2.at[k, j - 1], v2.at[k, j - 1])
             total = total + r2[k, j - 1].astype(F32)
         s2[k] = total.astype(BF16)
-        send(s2.at[k, :, 1 - x], r3.at[k], t3.at[k], v3.at[k], across)
+        push(s2.at[k, :, 1 - x], r3.at[k], t3.at[k], v3.at[k], across)
 
     def stage_z(k):
         arrived(r3.at[k], v3.at[k])
         s3[k] = (s2[k, :, x].astype(F32) + r3[k].astype(F32)).astype(BF16)
         for j in range(1, half):
             peer = lax.rem(z + j, half)
-            send(s3.at[k, peer], r4.at[k, j - 1], t4.at[k, j - 1], v4.at[k, j - 1], (2 * peer + x, c))
+            push(s3.at[k, peer], r4.at[k, j - 1], t4.at[k, j - 1], v4.at[k, j - 1], (2 * peer + x, c))
 
     def stage_cand(k):
         total = s3[k, z].astype(F32)
@@ -361,53 +312,125 @@
             total = total + r4[k, j - 1].astype(F32)
         fin[k, c] = total.astype(BF16)
         for j in range(1, m):
-            send(fin.at[k, c], fin.at[k, c], t5.at[k, j - 1], v5.at[k, j - 1], cands[j - 1])
-
-    stages = (stage_x, stage_z, stage_cand)
-    for k in range(chunks):
-        stage_y(k)
-    for t in range(chunks + 2):
-        for lag, stage in enumerate(stages):
-            if 0 <= t - lag < chunks:
-                stage(t - lag)
-    for k in range(chunks):
-        for j in range(1, m):
-            arrived(fin.at[k, lax.rem(c - j + m, m)], v5.at[k, j - 1])
-    part = jnp.zeros((8, lanes), F32)
-    for k in range(chunks):
-        block = fin[k].astype(F32).reshape(m * rows // 8, 8, lanes)
-        part = part + jnp.sum(block * block, axis=0)
-    sq[...] = part
-    r6[d] = part
-    for j in range(1, n):
-        send(sq, r6.at[d], t6.at[j - 1], v6.at[j - 1], dps[j - 1])
-    for j in range(1, n):
-        arrived(r6.at[lax.rem(d - j + n, n)], v6.at[j - 1])
-    count = chunks * m * lanes * n * rows
-    squares = jnp.sum(jnp.sum(jnp.sum(r6[...], axis=0), axis=0, keepdims=True), axis=1, keepdims=True)
-    scale = 1.0 / (jnp.sqrt(squares / count) + EPS)
-    for k in range(chunks):
-        for i in range(m):
-            at = (k * m + i) * lanes
-            o_ref[:, at : at + lanes] = fin[k, i].astype(F32) * scale
-    for copy in copies:
-        copy.wait_send()
-
-
-def reduce_update(grads, n, m):
-    blocks, width, lanes = grads.shape
-    rows = width // n
-    duo, half = m // 2, n // 2
-    chunks = blocks // m
+            target = (d, lax.rem(c + j, m))
+            push(fin.at[k, c], fin.at[k, c], t5.at[k, j - 1], v5.at[k, j - 1], target)
+
+    stages = (stage_core, stage_y, stage_x, stage_z, stage_cand)
+    plan = stage_slots(duos, chunks * m, m)
+
+    def run(place):
+        for step in range(duos):
+            items = [item for item in plan if item[0] == 3 * step + place]
+            if items:
+
+                @pl.when(hp == step)
+                def _():
+                    for _, stage, k in items:
+                        stages[stage](k)
+
+    @pl.when(hp == 0)
+    def _():
+        greet([(d, lax.rem(c + j, m)) for j in range(1, m)] + [(lax.rem(d + j, n), c) for j in range(1, n)])
+        load = pltpu.make_async_copy(gvo_ref, grads.at[:duos], own)
+        load.start()
+        for i in range(pairs):
+            part = jnp.dot(wc_ref[i], nt_ref[:, i * seq : (i + 1) * seq], preferred_element_type=F32)
+            for j in range(duos):
+                dp_scr[j, i] = part[2 * j : 2 * j + 2]
+        load.wait()
+
+    run(0)
+    low, high = half_masks(span)
+
+    def pair(i, carry):
+        probs = p_ref[i].astype(F32)
+        term = probs * dp_scr[hp, i][:, None, :]
+        dlog = (term - probs * jnp.sum(term, axis=-1, keepdims=True)).astype(BF16)
+        wide = jnp.concatenate([dlog[0], dlog[1]], axis=1)
+        dq = jnp.dot(wide, stack_halves(k_ref[i], low, high), preferred_element_type=F32)
+        dk = lax.dot_general(
+            dlog.reshape(2 * seq, seq), stack_halves(q_ref[i], low, high), TN, preferred_element_type=F32
+        )
+        dqk_scr[i, :, :span] = dq.astype(BF16)
+        dqk_scr[i, :, span:] = dk.astype(BF16)
+        return carry
+
+    lax.fori_loop(0, pairs, pair, 0, unroll=4)
+    run(1)
+    grad = jnp.dot(nt_ref[...], dqk_scr[...].reshape(pairs * seq, 2 * span), preferred_element_type=F32)
+    grads[duos + hp, 0] = grad[:, :span].reshape(half, 2, rows, lanes).astype(BF16)
+    grads[duos + hp, 1] = grad[:, span:].reshape(half, 2, rows, lanes).astype(BF16)
+    run(2)
+
+    @pl.when(hp == duos - 1)
+    def _():
+        for slot, stage, k in plan:
+            if slot >= 3 * duos:
+                stages[stage](k)
+        for k in range(chunks):
+            for j in range(1, m):
+                arrived(fin.at[k, lax.rem(c - j + m, m)], v5.at[k, j - 1])
+        part = jnp.zeros((8, lanes), F32)
+        for k in range(chunks):
+            block = fin[k].astype(F32).reshape(m * rows // 8, 8, lanes)
+            part = part + jnp.sum(block * block, axis=0)
+        sq[...] = part
+        r6[d] = part
+        for j in range(1, n):
+            push(sq, r6.at[d], t6.at[j - 1], v6.at[j - 1], (lax.rem(d + j, n), c))
+        for j in range(1, n):
+            arrived(r6.at[lax.rem(d - j + n, n)], v6.at[j - 1])
+        count = chunks * m * lanes * n * rows
+        squares = jnp.sum(jnp.sum(jnp.sum(r6[...], axis=0), axis=0, keepdims=True), axis=1, keepdims=True)
+        scale = 1.0 / (jnp.sqrt(squares / count) + EPS)
+        for k in range(chunks):
+            for i in range(m):
+                at = k * m + i
+                if at < 2 * duos:
+                    at = 2 * duos + at
+                else:
+                    at = (at % 2) * duos + (at - 2 * duos) // 2
+                o_ref[:, at * lanes : (at + 1) * lanes] = fin[k, i].astype(F32) * scale
+        for k in range(chunks):
+            arrived(r1.at[k], t1.at[k])
+            arrived(r3.at[k], t3.at[k])
+            for j in range(duo - 1):
+                arrived(r2.at[k, j], t2.at[k, j])
+            for j in range(half - 1):
+                arrived(r4.at[k, j], t4.at[k, j])
+            for j in range(m - 1):
+                arrived(fin.at[k, c], t5.at[k, j])
+        for j in range(n - 1):
+            arrived(sq, t6.at[j])
+
+
+def backward(normed_t, qk, probs, wc, gvo, n, m):
+    pairs, heads, seq, _ = probs.shape
+    width = normed_t.shape[0]
+    lanes = 2 * (width // heads)
+    duos = heads // 2
+    rows, half, duo = width // n, n // 2, m // 2
+    chunks = 4 * duos // m
+    near, far = max(duo - 1, 1), max(half - 1, 1)
     dma = pltpu.SemaphoreType.DMA
     vmem = pltpu.VMEM
-    near, far = max(duo - 1, 1), max(half - 1, 1)
     return pl.pallas_call(
-        functools.partial(reduce_kernel, n, m),
-        in_specs=[pl.BlockSpec(memory_space=pltpu.VMEM)],
-        out_specs=pl.BlockSpec(memory_space=pltpu.VMEM),
-        out_shape=jax.ShapeDtypeStruct((rows, blocks * lanes), F32),
+        functools.partial(backward_kernel, n, m),
+        grid=(duos,),
+        in_specs=[
+            pl.BlockSpec((width, pairs * seq), lambda h: (0, 0)),
+            pl.BlockSpec((pairs, seq, lanes), lambda h: (0, 0, h)),
+            pl.BlockSpec((pairs, seq, lanes), lambda h: (0, 0, duos + h)),
+            pl.BlockSpec((pairs, 2, seq, seq), lambda h: (0, h, 0, 0)),
+            pl.BlockSpec(wc.shape, lambda h: (0, 0, 0)),
+            pl.BlockSpec(memory_space=pl.ANY),
+        ],
+        out_specs=pl.BlockSpec((rows, 4 * width), lambda h: (0, 0)),
+        out_shape=jax.ShapeDtypeStruct((rows, 4 * width), F32),
         scratch_shapes=[
+            vmem((duos, pairs, 2, seq), F32),
+            vmem((pairs, seq, 2 * lanes), BF16),
+            vmem((2 * duos, 2, half, 2, rows, lanes), BF16),
             vmem((chunks, duo, half, 2, rows, lanes), BF16),
             vmem((chunks, duo, half, 2, rows, lanes), BF16),
             vmem((chunks, near, half, 2, rows, lanes), BF16),
@@ -418,6 +441,7 @@
             vmem((chunks, m, rows, lanes), BF16),
             vmem((8, lanes), F32),
             vmem((n, 8, lanes), F32),
+            pltpu.SemaphoreType.DMA,
             dma((chunks,)), dma((chunks,)),
             dma((chunks, near)), dma((chunks, near)),
             dma((chunks,)), dma((chunks,)),
@@ -428,8 +452,9 @@
         compiler_params=pltpu.CompilerParams(
             collective_id=1, has_side_effects=True, vmem_limit_bytes=VMEM_LIMIT
         ),
-        name="reduce_update",
-    )(grads.reshape(chunks, duo, 2, half, 2, rows, lanes))
+        cost_estimate=pl.CostEstimate(flops=30_000_000_000, bytes_accessed=20_000_000, transcendentals=0),
+        name="backward_reduce",
+    )(normed_t, qk, qk, probs, wc, gvo.reshape(duos, 2, half, 2, rows, lanes))
 
 
 def shards(hidden, attn_weight, norm_gain, pos_bias, score_weight, pair_lengths, labels):
@@ -475,20 +500,19 @@
     target = jnp.exp(labels.astype(F32))
     score_grad = jnp.exp(scores - highest[:, None]) / expsum[:, None] - target / target_sum[:, None]
     duos, duo = heads // 2, 2 * head_size
-    wc, grads = pl.pallas_call(
+    wc, gvo = pl.pallas_call(
         functools.partial(middle_kernel, head_size),
         grid=(1,),
         in_specs=[col, wide, col, whole(1, width), whole(*u.shape), wide, w_spec],
-        out_specs=[whole(*u.shape), pl.BlockSpec((2, duos, width, duo), lambda i: (1, 0, 0, 0))],
+        out_specs=[whole(*u.shape), whole(2, duos, width, duo)],
         out_shape=[
             jax.ShapeDtypeStruct(u.shape, BF16),
-            jax.ShapeDtypeStruct((4, duos, width, duo), BF16),
+            jax.ShapeDtypeStruct((2, duos, width, duo), BF16),
         ],
         compiler_params=params,
         name="score_backward",
     )(score_grad.reshape(pairs, 1), pooled, len_col, sw, u, ctx, weights)
-    grads = backward(normed_t, qk, probs, wc, grads)
-    update = reduce_update(grads.reshape(4 * duos, width, duo), n, m)
+    update = backward(normed_t, qk, probs, wc, gvo, n, m)
     return (update, loss)
 
 

time: 174 us -> 157 us (0.902)
  Pallas kernels: 156 us -> 138 us
    pallas_call x2 -> x1, Pallas kernels: 79.1 us -> 61.4 us  [backward(): pl.pallas_call(functools.partial(backward_kernel, n, m), grid=(duos,), in...]
where the time goes in v3:
time: 157 us; the launch traced here: 156 us
  Pallas kernels  138 us (88%)
  local copies, waits for them, and re-layouts  9.37 us (6%)
  blocking collectives  5.17 us (3%)
  other arithmetic  3.04 us (2%)
    pallas_call x1, Pallas kernels, backward(): pl.pallas_call(functools.partial(backward_kernel, n, m), grid=(duos,), in...  61.4 us
    pallas_call x1, Pallas kernels, gather_weights(): pl.pallas_call(functools.partial(gather_kernel, n, m), in_specs=[pl.Block...  40.8 us
    pallas_call x1, Pallas kernels, forward(): pl.pallas_call(functools.partial(forward_kernel, hpad), grid=(pairs // ba...  27.4 us
    all_gather x1, blocking collectives, shards(): every = lax.all_gather(mine, 'cand', axis=2, tiled=True)  5.17 us
    pallas_call x1, Pallas kernels, shards(): pl.pallas_call(functools.partial(middle_kernel, head_size), grid=(1,), in...  5.03 us
    unnamed x4, local copies, waits for them, and re-layouts  3.79 us
    pallas_call x1, Pallas kernels, shards(): pl.pallas_call(functools.partial(score_kernel, head_size), grid=(1,), in_...  3.25 us

profile of v3, /device:TPU:0, one launch (start us, length us, event | category | flops | bytes accessed | tf_op | source)
XLA Modules:
  0.0 156.0 jit_solution(3299904564447423512)
XLA Ops:
  0.6 1.3 reshape.44.len_ref
  1.9 0.7 convert_element_type.17
  2.6 0.7 convert_bitcast_fusion
  3.3 1.3 reshape.48.sw_ref
  4.5 1.3 reshape.46.gain_ref
  5.8 0.7 convert_element_type.20.len_ref
  6.5 40.8 %gather_weights.1 = bf16[4,8,96,768]{3,2,1,0:T(8,128)(2,1)} custom-call(bf16[96,3072]{1,0:T(8,128)(2,1)} %x_ref.1), custom_call_target="tpu_custom_call" | custom-call | tf_op jit(solution)/shard_map/gather_weights/pallas_call | solution.py:239
  47.3 27.4 %attend_forward.1 = (bf16[768,2048]{1,0:T(8,128)(2,1)}, bf16[16,128,1536]{2,1,0:T(8,128)(2,1)}, bf16[16,12,128,128]{3,2,1,0:T(8,128)(2,1)}, bf16[16,16,768]{2,1,0:T(8,128)(2,1)}, f32[16,1,768]{2,1,0:T(1,128)}) custom-call(s32[16]{0:T(128)} %reshape.44.len_ref, bf16[16,128,768]{2,1,0:T(8,128)(2,1)} %bitcast.23, f32[1,768]{1,0:T(1,128)} %reshape.46.gain_ref, ...), custom_call_target="tpu_custom_call" | custom-call | flops 30000001024 | bytes 24000000 | tf_op jit(solution)/shard_map/attend_forward/pallas_call | solution.py:79
  74.6 0.0 copy-start
  74.6 1.4 copy.23
  76.1 3.2 %score_forward.1 = (bf16[16,768]{1,0:T(8,128)(2,1)}, f32[16,768]{1,0:T(8,128)}, f32[16,1]{1,0:T(8,128)}) custom-call(bf16[16,16,768]{2,1,0:T(8,128)(2,1)} %get-tuple-element.15.u_ref, bf16[4,768,768]{2,1,0:T(8,128)(2,1)} %bitcast.20, f32[16,768]{1,0:T(8,128)} %bitcast.22, f32[16,1]{1,0:T(8,128)} %convert_element_type.20.len_ref, f32[1,768]{1,0:T(1,128)} %reshape.48.sw_ref), custom_call_target="tpu_custom_call" | custom-call | tf_op jit(solution)/shard_map/score_forward/pallas_call | solution.py:478
  79.3 0.8 reduce.2
  80.1 0.1 stack_reshape.3
  80.2 0.1 reshape.49
  80.3 0.1 copy.16
  80.4 5.2 %all_gather.3 = f32[2,2,32]{1,0,2:T(2,128)S(1)} all-gather(f32[2,2,8]{1,0,2:T(2,128)S(1)} %copy.16), channel_id=1, replica_groups=mesh['dp'=8,'cand'=4] {'cand'}, dimensions={2}, use_global_device_ids=true | all-gather | bytes 640 | tf_op jit(solution)/shard_map/all_gather | solution.py:493
  85.6 0.1 fusion.3
  85.6 0.1 copy.20
  85.7 0.1 copy.17
  85.8 0.2 fusion
  86.0 0.5 divide_subtract_fusion.1
  86.5 0.0 copy-done
  86.5 0.1 divide_subtract_fusion
  86.6 0.7 reshape.52.sg_ref
  87.3 5.0 %score_backward.1 = (bf16[16,16,768]{2,1,0:T(8,128)(2,1)}, bf16[2,6,768,128]{3,2,1,0:T(8,128)(2,1)}) custom-call(f32[16,1]{1,0:T(8,128)} %reshape.52.sg_ref, f32[16,768]{1,0:T(8,128)} %get-tuple-element.18.pooled_ref, f32[16,1]{1,0:T(8,128)} %convert_element_type.20.len_ref, f32[1,768]{1,0:T(1,128)} %reshape.48.sw_ref, ...), custom_call_target="tpu_custom_call" | custom-call | tf_op jit(solution)/shard_map/score_backward/pallas_call | solution.py:503
  92.3 61.4 %backward_reduce.1 = f32[96,3072]{1,0:T(8,128)} custom-call(bf16[768,2048]{1,0:T(8,128)(2,1)} %get-tuple-element.12.nt_ref, bf16[16,128,1536]{2,1,0:T(8,128)(2,1)} %get-tuple-element.13.q_ref.k_ref, bf16[16,128,1536]{2,1,0:T(8,128)(2,1)} %get-tuple-element.13.q_ref.k_ref, bf16[16,12,128,128]{3,2,1,0:T(8,128)(2,1)} %get-tuple-element.14.p_ref, ...), custom_call_target="tpu_custom_call" | custom-call | flops 30000001024 | bytes 20000000 | tf_op jit(solution)/shard_map/backward_reduce/pallas_call | solution.py:417
  153.7 2.4 %copy.25 = f32[96,3072]{1,0:T(8,128)} copy(f32[96,3072]{1,0:T(8,128)} %backward_reduce.1) | data formatting | bytes 2359296
  (1 shorter events, 0.0 us)
Async XLA Ops:
  74.6 11.9 %copy-start = (s32[2,8]{1,0:T(2,128)S(1)}, s32[2,8]{1,0:T(2,128)}, u32[]{:S(2)}) copy-start(s32[2,8]{1,0:T(2,128)} %param.13) | copy-start | bytes 196
